TPU v7x, 256 devices: a whole 4x4x8 slice. The times are simulated.
256 devices in a mesh: tile: 32 (over y, z_lo, core), depth: 8 (over z_hi, x).
Axes of the slice: x: 4, y: 4, z: 8 (z_hi: 2, z_lo: 4; z = z_hi * 4 + z_lo), core: 2. Of those that a mesh axis runs over, the one named last changes fastest.
Arguments:
- volume: float32 [64, 64, 256, 256], P('tile', 'depth'), may hold values from 0 to 1
- transfer: float32 [64, 2, 256, 256], P('depth', None, 'tile'), may hold values from -0.9 to 0.9
- measured: float32 [64, 256, 256], P('tile'), may hold values from 0.5 to 4
- background: float32 [64, 256, 256], P('tile'), may hold values from 1 to 4
- margins: int32 [64], replicated, may hold values from 8 to 32
- phases: int32 [64], P('depth'), may hold values from 0 to 255
Outputs:
- blended: float32 [64, 64, 256, 256], P('tile', 'depth')
All inputs are finite; a program needn't handle non-finite values.
Results may differ from a plain program's by a relative error of at most 0.00005.
Values sent between devices are 32-bit elements; how exact they have to be, the bound alone decides.
A program may use at most 128 MiB of HBM per device.

v0:
```python
import math

import jax
import jax.numpy as jnp
from jax import lax
from jax.sharding import PartitionSpec as P

INTERSECTION = 32


floor_level = 0.5
step_gain = 2.0
highest = lax.Precision.HIGHEST


def with_halo(cells, sides, width):
    for axis, dim in sides:
        count = lax.axis_size(axis)
        head = lax.slice_in_dim(cells, 0, width, axis=dim)
        tail = lax.slice_in_dim(cells, cells.shape[dim] - width, cells.shape[dim], axis=dim)
        cells = jnp.concatenate(
            [
                lax.ppermute(tail, axis, [(i, (i + 1) % count) for i in range(count)]),
                cells,
                lax.ppermute(head, axis, [((i + 1) % count, i) for i in range(count)]),
            ],
            axis=dim,
        )
    return cells


def tables(side):
    places = lax.iota(jnp.int32, side)
    angle = (places[:, None] * places[None, :] % side).astype(jnp.float32) * (2.0 * math.pi / side)
    return (jnp.cos(angle), jnp.sin(angle))


def times_left(matrix, table):
    return jnp.matmul(table, matrix, precision=highest)


def times_right(matrix, table):
    return jnp.matmul(matrix, table, precision=highest)


def forward_transform(values, cos_table, sin_table):
    half_real = times_left(values, cos_table)
    half_imag = -times_left(values, sin_table)
    real_part = times_right(half_real, cos_table) + times_right(half_imag, sin_table)
    imag_part = times_right(half_imag, cos_table) - times_right(half_real, sin_table)
    return (real_part, imag_part)


def inverse_real(real_part, imag_part, cos_table, sin_table):
    side = cos_table.shape[0]
    half_real = times_left(real_part, cos_table) - times_left(imag_part, sin_table)
    half_imag = times_left(imag_part, cos_table) + times_left(real_part, sin_table)
    return (times_right(half_real, cos_table) - times_right(half_imag, sin_table)) / float(
        side * side
    )


def rotate_rows(piece, phases):
    side = piece.shape[-1]
    columns = lax.iota(jnp.int32, side)
    angle = (phases[:, None] * columns[None, :] % side).astype(jnp.float32) * (2.0 * math.pi / side)
    cosine = jnp.cos(angle)[:, None, :]
    sine = jnp.sin(angle)[:, None, :]
    real_part = piece[:, 0]
    imag_part = piece[:, 1]
    return (real_part * cosine + imag_part * sine, imag_part * cosine - real_part * sine)


def ramp_weights(margin_values):
    width = INTERSECTION
    offsets = lax.iota(jnp.float32, width)
    margin_float = margin_values.astype(jnp.float32)[:, None]
    return jnp.clip(
        (offsets[None, :] + 0.5 - (width - margin_float) / 2.0) / margin_float, 0.0, 1.0
    )


def on_device(volume, transfer, measured, background, margins, phases):
    side = volume.shape[-1]
    width = INTERSECTION
    local_tiles = volume.shape[0]
    cos_table, sin_table = tables(side)
    spec_real, spec_imag = forward_transform(volume, cos_table, sin_table)
    gathered = lax.all_gather(transfer, "tile", axis=2, tiled=True)
    trans_real, trans_imag = rotate_rows(gathered, phases)
    part_real = spec_real
    part_imag = spec_imag
    sum_real = jnp.sum(part_real * trans_real[None] - part_imag * trans_imag[None], axis=1)
    sum_imag = jnp.sum(part_real * trans_imag[None] + part_imag * trans_real[None], axis=1)
    spectrum = jnp.stack((sum_real, sum_imag), axis=1)
    partial_image = inverse_real(spectrum[:, 0], spectrum[:, 1], cos_table, sin_table)
    image = lax.psum(partial_image, "depth")
    projection = background + image
    ratio = measured / jnp.maximum(projection, floor_level)
    ratio_real, ratio_imag = forward_transform(ratio - 1.0, cos_table, sin_table)
    trans_real, trans_imag = rotate_rows(gathered, phases)
    part_real = ratio_real[:, None]
    part_imag = ratio_imag[:, None]
    back_real = trans_real[None] * part_real + trans_imag[None] * part_imag
    back_imag = trans_real[None] * part_imag - trans_imag[None] * part_real
    backward = jnp.stack((back_real, back_imag), axis=2)
    correction = inverse_real(backward[:, :, 0], backward[:, :, 1], cos_table, sin_table)
    updated = jnp.maximum(volume * (1.0 + step_gain * correction), 0.0)
    first_top = updated[0, :, :width]
    last_bottom = updated[local_tiles - 1, :, side - width :]
    outer_rows = with_halo(jnp.stack((first_top, last_bottom)), (("tile", 0),), 1)
    from_before = outer_rows[0]
    from_after = outer_rows[3]
    bottoms = updated[:, :, side - width :]
    tops = updated[:, :, :width]
    prev_bottoms = jnp.concatenate([from_before[None], bottoms[: local_tiles - 1]], axis=0)
    next_tops = jnp.concatenate([tops[1:], from_after[None]], axis=0)
    base = lax.axis_index("tile") * local_tiles
    own_margins = lax.dynamic_slice_in_dim(margins, base, local_tiles, 0)
    shifted_margins = jnp.concatenate([margins[margins.shape[0] - 1 :], margins], axis=0)
    prev_margins = lax.dynamic_slice_in_dim(shifted_margins, base, local_tiles, 0)
    weight_own = ramp_weights(own_margins)[:, None, :, None]
    weight_prev = ramp_weights(prev_margins)[:, None, :, None]
    new_bottom = (1.0 - weight_own) * bottoms + weight_own * next_tops
    new_top = (1.0 - weight_prev) * prev_bottoms + weight_prev * tops
    return jnp.concatenate([new_top, updated[:, :, width : side - width], new_bottom], axis=2)


def solution(mesh):
    return jax.shard_map(
        on_device,
        mesh=mesh,
        in_specs=(
            P("tile", "depth", None, None),
            P("depth", None, "tile", None),
            P("tile", None, None),
            P("tile", None, None),
            P(),
            P("depth"),
        ),
        out_specs=P("tile", "depth", None, None),
        check_vma=False,
    )
```

profile of v0, /device:TPU:6, one launch (start us, length us, event | category | flops | bytes accessed | tf_op | source)
XLA Modules:
  0.0 269.8 jit_solution(1053794502332086961)
XLA Ops:
  7.3 0.8 fusion.120
  8.1 8.1 %fusion.64 = f32[256,2,8,256]{3,0,2,1:T(8,128)S(1)} fusion(f32[2,8,256,256]{3,2,1,0:T(8,128)} %param.6), kind=kOutput, calls=%fused_computation.83 | convolution fusion | flops 3222142976 | bytes 8388608 | tf_op jit(solution)/shard_map/dot_general | solution.py:39
  16.2 4.7 %fusion.71 = f32[256,2,8,256]{3,0,2,1:T(8,128)S(1)} fusion(f32[2,8,256,256]{3,2,1,0:T(8,128)S(1)} %copy-done.2), kind=kOutput, calls=%fused_computation.90 | convolution fusion | flops 3222142976 | bytes 8388608 | tf_op jit(solution)/shard_map/dot_general | solution.py:39
  20.9 4.4 %fusion.6 = f32[2,8,256,256]{3,2,1,0:T(8,128)S(1)} fusion(f32[256,2,8,256]{3,0,2,1:T(8,128)S(1)} %fusion.64), kind=kOutput, calls=%fused_computation.7 | convolution fusion | flops 3223191552 | bytes 8388608 | tf_op jit(solution)/shard_map/dot_general | solution.py:43
  25.4 7.1 %fusion.4 = f32[2,8,256,256]{3,2,1,0:T(8,128)} fusion(f32[256,2,8,256]{3,0,2,1:T(8,128)S(1)} %fusion.64), kind=kOutput, calls=%fused_computation.5 | convolution fusion | flops 3223191552 | bytes 8388608 | tf_op jit(solution)/shard_map/dot_general | solution.py:43
  32.4 7.1 %fusion.20 = f32[2,8,256,256]{3,2,1,0:T(8,128)} fusion(f32[2,8,256,256]{3,2,1,0:T(8,128)S(1)} %fusion.6, f32[256,2,8,256]{3,0,2,1:T(8,128)S(1)} %fusion.71), kind=kOutput, calls=%fused_computation.26 | convolution fusion | flops 3223191552 | bytes 12582912 | tf_op jit(solution)/shard_map/dot_general | solution.py:43
  39.5 35.0 %all-gather.2.cloned.1.call-done = f32[8,2,256,256]{3,2,1,0:T(8,128)} async-done(((f32[8,2,8,256]{3,2,1,0:T(8,128)}), f32[8,2,256,256]{3,2,1,0:T(8,128)}) %all-gather.2.cloned.1.call-update) | async-done | bytes 4194320 | tf_op jit(solution)/shard_map/all_gather | solution.py:89
  74.5 2.9 %multiply_add_fusion.3 = (f32[8,256,256]{2,1,0:T(8,128)S(1)}, f32[8,256,256]{2,1,0:T(8,128)S(1)}) fusion(f32[8,2,256,256]{3,2,1,0:T(8,128)} %all-gather.2.cloned.1.call-done, f32[8,256]{1,0:T(8,128)S(1)} %get-tuple-element.26, f32[8,256]{1,0:T(8,128)S(1)} %get-tuple-element.25), kind=kLoop, calls=%fused_computation.47 | loop fusion | flops 3145728 | bytes 8404992 | tf_op jit(solution)/shard_map/add | solution.py:71
  78.0 2.0 copy-done.6
  80.0 7.7 %add_reduce_fusion = (f32[2,256,256]{2,1,0:T(8,128)S(1)}, f32[2,256,256]{2,1,0:T(8,128)S(1)}) fusion(f32[2,8,256,256]{3,2,1,0:T(8,128)S(1)} %copy-done.6, f32[8,256,256]{2,1,0:T(8,128)S(1)} %get-tuple-element.16, f32[8,256,256]{2,1,0:T(8,128)S(1)} %get-tuple-element.15, f32[2,8,256,256]{3,2,1,0:T(8,128)} %fusion.4, f32[256,2,8,256]{3,0,2,1:T(8,128)S(1)} %copy-done.5), kind=kOutput, calls=%fused_computation.22 | convolution fusion | flops 3231318016 | bytes 17825792 | tf_op jit(solution)/shard_map/dot_general | solution.py:43
  87.8 1.6 fusion.82
  89.4 1.6 fusion.78
  91.1 1.6 fusion.47
  92.7 2.0 fusion.80
  94.7 1.6 fusion.46
  96.3 2.4 fusion.45
  100.1 104.7 %all-reduce.2.cloned.1.call-done = f32[2,256,256]{2,1,0:T(8,128)} async-done(((f32[2,256,256]{2,1,0:T(8,128)}), f32[2,256,256]{2,1,0:T(8,128)}) %all-reduce.2.cloned.1.call-update) | async-done | bytes 524304 | tf_op jit(solution)/shard_map/psum | solution.py:97
  204.8 2.8 %fusion.44 = f32[2,256,256]{2,1,0:T(8,128)S(1)} fusion(f32[2,256,256]{2,1,0:T(8,128)S(1)} %copy-done.8, f32[2,256,256]{2,1,0:T(8,128)S(1)} %copy-done.9, f32[2,256,256]{2,1,0:T(8,128)} %all-reduce.2.cloned.1.call-done), kind=kOutput, calls=%fused_computation.49 | convolution fusion | flops 404226048 | bytes 2097152 | tf_op jit(solution)/shard_map/dot_general | solution.py:39
  207.7 1.6 fusion.73
  209.3 1.7 convolution_bitcast_fusion
  211.0 1.6 fusion.75
  212.6 1.7 convolution_subtract_fusion
  214.3 1.6 convolution_add_fusion
  215.9 5.4 %fusion.14 = f32[256,2,8,256]{3,0,2,1:T(8,128)S(1)} fusion(f32[2,256,256]{2,1,0:T(8,128)S(1)} %convolution_subtract_fusion, f32[2,256,256]{2,1,0:T(8,128)S(1)} %convolution_add_fusion, f32[8,256,256]{2,1,0:T(8,128)S(1)} %copy-done.1, f32[8,256,256]{2,1,0:T(8,128)S(1)} %get-tuple-element.15), kind=kOutput, calls=%fused_computation.17 | convolution fusion | flops 3225288704 | bytes 9437184 | tf_op jit(solution)/shard_map/dot_general | solution.py:39
  221.3 5.4 %fusion.16 = f32[256,2,8,256]{3,0,2,1:T(8,128)S(1)} fusion(f32[2,256,256]{2,1,0:T(8,128)S(1)} %convolution_subtract_fusion, f32[2,256,256]{2,1,0:T(8,128)S(1)} %convolution_add_fusion, f32[8,256,256]{2,1,0:T(8,128)S(1)} %copy-done.1, f32[8,256,256]{2,1,0:T(8,128)S(1)} %get-tuple-element.15), kind=kOutput, calls=%fused_computation.20 | convolution fusion | flops 3225288704 | bytes 9437184 | tf_op jit(solution)/shard_map/dot_general | solution.py:39
  226.8 5.6 %fusion.17 = f32[256,2,8,256]{3,0,2,1:T(8,128)S(1)} fusion(f32[2,256,256]{2,1,0:T(8,128)S(1)} %convolution_subtract_fusion, f32[2,256,256]{2,1,0:T(8,128)S(1)} %convolution_add_fusion, f32[8,256,256]{2,1,0:T(8,128)S(1)} %copy-done.1, f32[8,256,256]{2,1,0:T(8,128)S(1)} %get-tuple-element.15), kind=kOutput, calls=%fused_computation.21 | convolution fusion | flops 3225288704 | bytes 9437184 | tf_op jit(solution)/shard_map/dot_general | solution.py:39
  232.4 5.4 %fusion.15 = f32[256,2,8,256]{3,0,2,1:T(8,128)S(1)} fusion(f32[2,256,256]{2,1,0:T(8,128)S(1)} %convolution_subtract_fusion, f32[2,256,256]{2,1,0:T(8,128)S(1)} %convolution_add_fusion, f32[8,256,256]{2,1,0:T(8,128)S(1)} %copy-done.1, f32[8,256,256]{2,1,0:T(8,128)S(1)} %get-tuple-element.15), kind=kOutput, calls=%fused_computation.18 | convolution fusion | flops 3225288704 | bytes 9437184 | tf_op jit(solution)/shard_map/dot_general | solution.py:39
  237.8 4.9 %fusion = f32[2,8,256,256]{3,2,1,0:T(8,128)S(1)} fusion(f32[256,2,8,256]{3,0,2,1:T(8,128)S(1)} %fusion.14, f32[256,2,8,256]{3,0,2,1:T(8,128)S(1)} %fusion.16), kind=kOutput, calls=%fused_computation.1 | convolution fusion | flops 3223191552 | bytes 12582912 | tf_op jit(solution)/shard_map/dot_general | solution.py:43
  242.7 5.1 %multiply_maximum_fusion = f32[2,8,256,256]{3,2,1,0:T(8,128)S(1)} fusion(f32[2,8,256,256]{3,2,1,0:T(8,128)S(1)} %copy-done.3, f32[2,8,256,256]{3,2,1,0:T(8,128)S(1)} %fusion, f32[256,2,8,256]{3,0,2,1:T(8,128)S(1)} %fusion.17, f32[256,2,8,256]{3,0,2,1:T(8,128)S(1)} %fusion.15), kind=kOutput, calls=%fused_computation.13 | convolution fusion | flops 3228434432 | bytes 20971520 | tf_op jit(solution)/shard_map/dot_general | solution.py:43
  247.9 5.6 %collective-permute-start.1 = (f32[1,8,32,256]{3,2,1,0:T(8,128)S(1)}, f32[1,8,32,256]{3,2,1,0:T(8,128)S(1)}, u32[]{:S(2)}, u32[]{:S(2)}) collective-permute-start(f32[1,8,32,256]{3,2,1,0:T(8,128)S(1)} %get-tuple-element.20), channel_id=1, source_target_pairs={{8,0},{16,8},{24,16},{32,24},{40,32},{48,40},{56,48},{64,56},{72,6... | collective-permute-start | bytes 786440 | tf_op jit(solution)/shard_map/ppermute | solution.py:25
  253.9 6.1 %collective-permute-done = f32[1,8,32,256]{3,2,1,0:T(8,128)S(1)} collective-permute-done((f32[1,8,32,256]{3,2,1,0:T(8,128)S(1)}, f32[1,8,32,256]{3,2,1,0:T(8,128)S(1)}, u32[]{:S(2)}, u32[]{:S(2)}) %collective-permute-start) | collective-permute-done | bytes 262176 | tf_op jit(solution)/shard_map/ppermute | solution.py:23
  260.2 2.3 pad_maximum_fusion
  (35 shorter events, 3.4 us)
Async XLA Ops:
  6.5 68.0 %all-gather.2.cloned.1.call-start = ((), (), s32[]{:S(2)}) async-start(), calls=%async_computation | async-start | bytes 4325376 | tf_op jit(solution)/shard_map/all_gather | solution.py:89
  7.3 197.6 %all-reduce.2.cloned.1.call-start = ((), (), s32[]{:S(2)}) async-start(), calls=%async_computation.1 | async-start | bytes 1048576 | tf_op jit(solution)/shard_map/psum | solution.py:97
  8.1 8.1 %copy-start.2 = (f32[2,8,256,256]{3,2,1,0:T(8,128)S(1)}, f32[2,8,256,256]{3,2,1,0:T(8,128)}, u32[]{:S(2)}) copy-start(f32[2,8,256,256]{3,2,1,0:T(8,128)} %param.6) | copy-start | bytes 12582916
  20.9 11.5 %copy-start.4 = (f32[256,2,8,256]{3,0,2,1:T(8,128)}, f32[256,2,8,256]{3,0,2,1:T(8,128)S(1)}, u32[]{:S(2)}) copy-start(f32[256,2,8,256]{3,0,2,1:T(8,128)S(1)} %fusion.71) | copy-start | bytes 12582916
  74.5 3.5 %copy-start.5 = (f32[256,2,8,256]{3,0,2,1:T(8,128)S(1)}, f32[256,2,8,256]{3,0,2,1:T(8,128)}, u32[]{:S(2)}) copy-start(f32[256,2,8,256]{3,0,2,1:T(8,128)} %copy-done.4) | copy-start | bytes 12582916
  74.5 5.5 %copy-start.6 = (f32[2,8,256,256]{3,2,1,0:T(8,128)S(1)}, f32[2,8,256,256]{3,2,1,0:T(8,128)}, u32[]{:S(2)}) copy-start(f32[2,8,256,256]{3,2,1,0:T(8,128)} %fusion.20) | copy-start | bytes 12582916
  77.5 10.2 %copy-start = (f32[8,256,256]{2,1,0:T(8,128)}, f32[8,256,256]{2,1,0:T(8,128)S(1)}, u32[]{:S(2)}) copy-start(f32[8,256,256]{2,1,0:T(8,128)S(1)} %get-tuple-element.16) | copy-start | bytes 6291460
  87.7 10.9 %copy-start.7 = (s32[64]{0:T(128)S(1)}, s32[64]{0:T(128)}, u32[]{:S(2)}) copy-start(s32[64]{0:T(128)} %param.10) | copy-start | bytes 772
  87.8 117.1 %copy-start.8 = (f32[2,256,256]{2,1,0:T(8,128)S(1)}, f32[2,256,256]{2,1,0:T(8,128)}, u32[]{:S(2)}) copy-start(f32[2,256,256]{2,1,0:T(8,128)} %param.8) | copy-start | bytes 1572868
  87.8 117.1 %copy-start.9 = (f32[2,256,256]{2,1,0:T(8,128)S(1)}, f32[2,256,256]{2,1,0:T(8,128)}, u32[]{:S(2)}) copy-start(f32[2,256,256]{2,1,0:T(8,128)} %param.9) | copy-start | bytes 1572868
  204.8 4.4 %copy-start.10 = (f32[2,256,256]{2,1,0:T(8,128)S(1)}, f32[2,256,256]{2,1,0:T(8,128)}, u32[]{:S(2)}) copy-start(f32[2,256,256]{2,1,0:T(8,128)} %all-reduce.2.cloned.1.call-done) | copy-start | bytes 1572868
  207.7 8.2 %copy-start.1 = (f32[8,256,256]{2,1,0:T(8,128)S(1)}, f32[8,256,256]{2,1,0:T(8,128)}, u32[]{:S(2)}) copy-start(f32[8,256,256]{2,1,0:T(8,128)} %copy-done) | copy-start | bytes 6291460
  237.8 4.9 %copy-start.3 = (f32[2,8,256,256]{3,2,1,0:T(8,128)S(1)}, f32[2,8,256,256]{3,2,1,0:T(8,128)}, u32[]{:S(2)}) copy-start(f32[2,8,256,256]{3,2,1,0:T(8,128)} %param.6) | copy-start | bytes 12582916
  247.8 12.2 %collective-permute-start = (f32[1,8,32,256]{3,2,1,0:T(8,128)S(1)}, f32[1,8,32,256]{3,2,1,0:T(8,128)S(1)}, u32[]{:S(2)}, u32[]{:S(2)}) collective-permute-start(f32[1,8,32,256]{3,2,1,0:T(8,128)S(1)} %get-tuple-element.19), channel_id=1, source_target_pairs={{0,8},{8,16},{16,24},{24,32},{32,40},{40,48},{48,56},{56,64},{64,7... | collective-permute-start | bytes 786440 | tf_op jit(solution)/shard_map/ppermute | solution.py:23
  247.9 12.1 %collective-permute-start.1 = (f32[1,8,32,256]{3,2,1,0:T(8,128)S(1)}, f32[1,8,32,256]{3,2,1,0:T(8,128)S(1)}, u32[]{:S(2)}, u32[]{:S(2)}) collective-permute-start(f32[1,8,32,256]{3,2,1,0:T(8,128)S(1)} %get-tuple-element.20), channel_id=1, source_target_pairs={{8,0},{16,8},{24,16},{32,24},{40,32},{48,40},{56,48},{64,56},{72,6... | collective-permute-start | bytes 786440 | tf_op jit(solution)/shard_map/ppermute | solution.py:25
Sparse Core Ops, SparseCore 0:
  9.2 65.2 all-gather.1
  98.8 105.9 all-reduce.1
where the time goes:
time: 273 us; the launch traced here: 270 us
  waiting for transfers between devices  147 us (54%)
  matrix products  92.7 us (34%)
  between operations  14.2 us (5%)
  other arithmetic  7.14 us (3%)
  starting transfers between devices  5.76 us (2%)
  local copies, waits for them, and re-layouts  3.52 us (1%)
    psum x1, waiting for transfers between devices, on_device(): image = lax.psum(partial_image, 'depth')  105 us
    dot_general x12, matrix products, times_right(): return jnp.matmul(matrix, table, precision=highest)  46.9 us
    dot_general x12, matrix products, times_left(): return jnp.matmul(table, matrix, precision=highest)  45.7 us
    all_gather x1, waiting for transfers between devices, on_device(): gathered = lax.all_gather(transfer, 'tile', axis=2, tiled=True)  35 us
    ppermute x1, waiting for transfers between devices, with_halo(): lax.ppermute(tail, axis, [(i, (i + 1) % count) for i in range(count)])  6.05 us
    ppermute x1, starting transfers between devices, with_halo(): lax.ppermute(head, axis, [((i + 1) % count, i) for i in range(count)])  5.64 us
  transfers between devices with their start and end apart: 4, of which 3 were waited for; matrix products, arithmetic and copies ran while one was open for 13% of the time, Pallas kernels for 0%

commit v1 on v0

v1 whole, which is shorter than its diff:
```python
import functools
import math

import jax
import jax.numpy as jnp
import numpy as np
from jax import lax
from jax.experimental import pallas as pl
from jax.experimental.pallas import tpu as pltpu
from jax.sharding import PartitionSpec as P

SIDE = 256
HALF = 128
WIDTH = 32
TILES = 64
LOCAL_TILES = 2
LOCAL_PLANES = 8
SUBS = 2
SUB_ROWS = 128 // SUBS
FLOOR_LEVEL = 0.5
STEP_GAIN = 2.0
MESH = pl.DeviceIdType.MESH
f32 = jnp.float32
bf16 = jnp.bfloat16


def packed_tables():
    place = np.arange(SIDE)
    table = np.zeros((SIDE, SIDE))
    for a in range(HALF):
        table[a] = np.cos(2 * np.pi * (a * place % SIDE) / SIDE)
    table[HALF] = 1.0 - 2.0 * (place % 2)
    for a in range(1, HALF):
        table[HALF + a] = np.sin(2 * np.pi * (a * place % SIDE) / SIDE)
    weight = np.full(SIDE, 2.0)
    weight[0] = weight[HALF] = 1.0
    inverse = table.T * weight / SIDE
    pieces = []
    for matrix in (table, table.T, inverse, inverse.T):
        high = matrix.astype(bf16)
        pieces += [high, (matrix - high.astype(np.float64)).astype(bf16)]
    return jnp.asarray(np.stack(pieces))


def pairing():
    move = np.zeros((HALF, HALF), np.float32)
    move[0, 0] = 1.0
    for b in range(1, HALF):
        move[HALF - b, b] = 1.0
    return jnp.asarray(move.astype(bf16))


def split(values):
    high = values.astype(bf16)
    return high, (values - high.astype(f32)).astype(bf16)


def dot(a, b):
    return jnp.dot(a, b, preferred_element_type=f32)


def dot3(a, b):
    return dot(a[0], b[0]) + dot(a[1], b[0]) + dot(a[0], b[1])


def special(shape, first):
    lane0 = lax.broadcasted_iota(jnp.int32, shape, 1) == 0
    row0 = None
    if first:
        row0 = jnp.logical_and(
            lax.broadcasted_iota(jnp.int32, shape, 0) == 0, jnp.logical_not(lane0)
        )
    return lane0, row0


def quads_in(cc, cs, sc, ss, first):
    lane0, row0 = special(cc.shape, first)
    pr, pi, mr, mi = cc - ss, cs + sc, cc + ss, cs - sc
    if first:
        pr = jnp.where(row0, cc, pr)
        pi = jnp.where(row0, cs, pi)
        mr = jnp.where(row0, sc, mr)
        mi = jnp.where(row0, ss, mi)
    return (
        jnp.where(lane0, cc, pr),
        jnp.where(lane0, sc, pi),
        jnp.where(lane0, cs, mr),
        jnp.where(lane0, ss, mi),
    )


def quads_out(pr, pi, mr, mi, first):
    lane0, row0 = special(pr.shape, first)
    cc, ss, cs, sc = pr + mr, mr - pr, pi + mi, pi - mi
    if first:
        cc = jnp.where(row0, pr, cc)
        cs = jnp.where(row0, pi, cs)
        sc = jnp.where(row0, mr, sc)
        ss = jnp.where(row0, mi, ss)
    return (
        jnp.where(lane0, pr, cc),
        jnp.where(lane0, mr, cs),
        jnp.where(lane0, pi, sc),
        jnp.where(lane0, mi, ss),
    )


def times(hr, hi, real, imag, first, conj):
    second = hr
    if first:
        lane0, _ = special(hr.shape, False)
        corner = jnp.logical_and(lane0, lax.broadcasted_iota(jnp.int32, hr.shape, 0) == 0)
        second = jnp.where(corner, hi, hr)
        hi = jnp.where(corner, 0.0, hi)
    if conj:
        return hr * real - hi * imag, second * imag + hi * real
    return hr * real + hi * imag, second * imag - hi * real


def ramp(margin):
    margin = margin.astype(f32)
    row = lax.broadcasted_iota(jnp.int32, (WIDTH, SIDE), 0).astype(f32)
    return jnp.clip((row + 0.5 - (WIDTH - margin) / 2.0) / margin, 0.0, 1.0)


def kernel(
    phases,
    margins,
    transfer,
    volume_hbm,
    measured_hbm,
    background_hbm,
    mats_hbm,
    pair_ref,
    out_hbm,
    vol,
    packed,
    table,
    mats,
    measured,
    background,
    halves,
    mine,
    other,
    other0,
    pos,
    neg,
    sums,
    image,
    scattered,
    zsend,
    zrecv,
    ratio,
    ratio_quads,
    quads,
    part_high,
    part_low,
    top_send,
    bottom_send,
    after_recv,
    before_recv,
    vol_sem,
    in_sem,
    ex_send,
    ex_recv,
    ag_send,
    ag_recv,
    rs_send,
    rs_recv,
    z_send,
    z_recv,
    xg_send,
    xg_recv,
    halo_send,
    halo_recv,
    out_sem,
):
    tile = lax.axis_index("tile")
    depth = lax.axis_index("depth")
    core = lax.rem(tile, 2)
    zlo = lax.rem(tile // 2, 4)
    yrow = tile // 8
    xpos = lax.rem(depth, 4)
    zhi = depth // 4
    negative = tile >= 16
    block = jnp.where(negative, 31 - tile, tile)

    def at(y, z, c):
        return lax.rem(y, 4) * 8 + lax.rem(z, 4) * 2 + c

    def xpeer(d):
        return zhi * 4 + lax.rem(xpos + d, 4)

    after = lax.rem(tile + 1, 32)
    before = lax.rem(tile + 31, 32)
    zpartner = (1 - zhi) * 4 + xpos

    volume_copies = []
    for p in range(LOCAL_PLANES):
        volume_copies.append(
            pltpu.make_async_copy(volume_hbm.at[:, p], vol.at[:, p], vol_sem.at[p])
        )
    local = [
        pltpu.make_async_copy(mats_hbm, mats, in_sem.at[0]),
        pltpu.make_async_copy(measured_hbm, measured, in_sem.at[1]),
        pltpu.make_async_copy(background_hbm, background, in_sem.at[2]),
    ]
    local[0].start()
    for copy in volume_copies:
        copy.start()
    local[1].start()
    local[2].start()

    barrier = pltpu.get_barrier_semaphore()

    def greet(t, d):
        pl.semaphore_signal(barrier, inc=1, device_id=(t, d), device_id_type=MESH)

    greet(31 - tile, depth)
    for dz in range(1, 4):
        greet(at(yrow, zlo + dz, core), depth)
    greet(at(yrow + 1, zlo, core), depth)
    greet(at(yrow + 3, zlo, core), depth)
    greet(at(yrow, zlo, 1 - core), depth)
    for d in range(1, 4):
        greet(tile, xpeer(d))
    greet(tile, zpartner)
    greet(after, depth)
    greet(before, depth)
    first_of = lax.rem(32 - tile, 16)
    last_to = jnp.where(tile == 16, 31, tile - 1)
    last_from = jnp.where(tile == 31, 16, tile + 1)
    row0_from = jnp.where(tile == 0, 16, 32 - tile)

    @pl.when(negative)
    def _():
        greet(first_of, depth)
        greet(last_to, depth)
        greet(last_from, depth)

    @pl.when(jnp.logical_not(negative))
    def _():
        greet(row0_from, depth)

    whole = transfer[...].reshape(LOCAL_PLANES * 2 * 8, SIDE)
    halves[0] = whole[:, :HALF]
    rest = whole[:, HALF:]
    high, low = split(rest)
    lowest = ((rest - high.astype(f32)) - low.astype(f32)).astype(bf16)
    move = pair_ref[...]
    halves[1] = dot(high, move) + dot(low, move) + dot(lowest, move)
    for r in range(8):
        to = jnp.where(negative, (8 - r) % 8, r)
        for ph in range(2):
            for e in range(2):
                for c in range(2):
                    piece = halves[e, pl.ds(ph * 64 + c * 8 + r, 4, stride=16), :]
                    mine[ph, to, pl.ds((e * 2 + c) * 4, 4), :] = piece

    pl.semaphore_wait(barrier, 14 + 2 * (tile // 16))

    def remote(src, dst, send, recv, t, d):
        return pltpu.make_async_remote_copy(
            src_ref=src,
            dst_ref=dst,
            send_sem=send,
            recv_sem=recv,
            device_id=(t, d),
            device_id_type=MESH,
        )

    rows7 = pl.ds(1, 7)
    row1 = pl.ds(0, 1)
    up_all = remote(mine.at[1], other, ex_send.at[0], ex_recv.at[0], 31 - tile, depth)
    down_rest = remote(
        mine.at[0, rows7], other.at[rows7], ex_send.at[0], ex_recv.at[0], 31 - tile, depth
    )
    down_first = remote(
        mine.at[0, row1], other.at[row1], ex_send.at[1], ex_recv.at[1], first_of, depth
    )
    down_last = remote(mine.at[1, row1], other0, ex_send.at[2], ex_recv.at[1], last_to, depth)

    @pl.when(jnp.logical_not(negative))
    def _():
        up_all.start()

    @pl.when(negative)
    def _():
        down_rest.start()
        down_first.start()
        down_last.start()

    left = lambda: (mats[0], mats[1])
    right = lambda: (mats[2], mats[3])
    inv_left = lambda: (mats[4], mats[5])
    inv_right = lambda: (mats[6], mats[7])
    local[0].wait()

    def forward(p, carry):
        pltpu.make_async_copy(volume_hbm.at[:, p], vol.at[:, p], vol_sem.at[p]).wait()
        for t in range(LOCAL_TILES):
            half = dot3(split(vol[t, p]), right())
            packed[t, p] = dot3(left(), split(half))
        return carry

    lax.fori_loop(0, 4, forward, 0)

    @pl.when(jnp.logical_not(negative))
    def _():
        down_rest.wait_recv()
        down_first.wait_recv()
        pos[...] = mine[0]
        neg[...] = other[...]

    @pl.when(negative)
    def _():
        up_all.wait_recv()
        down_last.wait_recv()
        pos[...] = other[...]
        neg[0] = other0[0]
        neg[1:8] = mine[1, 1:8]

    plane0 = jnp.where(negative, 4, 0)
    column = lax.broadcasted_iota(jnp.int32, (4, HALF), 1)
    row4 = lax.broadcasted_iota(jnp.int32, (4, HALF), 0)
    phase = jnp.zeros((4, HALF), jnp.int32)
    for q in range(4):
        phase = jnp.where(row4 == q, phases[plane0 + q], phase)
    lane0 = column == 0

    def rotor(columns):
        angle = ((phase * columns) & (SIDE - 1)).astype(f32) * (2.0 * math.pi / SIDE)
        return jnp.cos(angle), jnp.sin(angle)

    cos_p, sin_p = rotor(column)
    cos_m, sin_m = rotor(jnp.where(lane0, HALF, column))
    sin_m = jnp.where(lane0, 0.0, sin_m)
    is_first = block == 0
    for r in range(8):
        epr, epi, fpr, fpi = (pos[r, pl.ds(c * 4, 4), :] for c in range(4))
        enr, eni, fnr, fni = (neg[r, pl.ds(c * 4, 4), :] for c in range(4))
        hpr, hpi = 0.25 * (epr + fnr), 0.25 * (epi - fni)
        hmr, hmi = 0.25 * (enr + fpr), 0.25 * (eni - fpi)
        if r == 0:
            at0 = jnp.logical_and(is_first, jnp.logical_not(lane0))
            hpr = jnp.where(at0, 0.5 * (epr + fpr), hpr)
            hpi = jnp.where(at0, 0.5 * (epi - fpi), hpi)
            hmr = jnp.where(at0, 0.5 * (enr + fnr), hmr)
            hmi = jnp.where(at0, 0.5 * (eni - fni), hmi)
        lpr, lpi = 0.5 * (epr + enr), 0.5 * (epi - eni)
        lmr, lmi = 0.5 * (fpr + fnr), 0.5 * (fpi - fni)
        if r == 0:
            lpr, lpi = jnp.where(is_first, epr, lpr), jnp.where(is_first, enr, lpi)
            lmr, lmi = jnp.where(is_first, fpr, lmr), jnp.where(is_first, fnr, lmi)
        hpr, hpi = jnp.where(lane0, lpr, hpr), jnp.where(lane0, lpi, hpi)
        hmr, hmi = jnp.where(lane0, lmr, hmr), jnp.where(lane0, lmi, hmi)
        parts = (
            hpr * cos_p + hpi * sin_p,
            hpi * cos_p - hpr * sin_p,
            hmr * cos_m + hmi * sin_m,
            hmi * cos_m - hmr * sin_m,
        )
        for c in range(4):
            for q in range(4):
                table[tile, q, c, pl.ds(r, 1), :] = parts[c][q : q + 1]

    started = []

    def pass_on(which, t):
        copy = remote(
            table.at[which],
            table.at[which],
            ag_send.at[len(started)],
            ag_recv.at[which],
            t,
            depth,
        )
        copy.start()
        started.append(copy)

    def arrived(which):
        remote(
            table.at[which], table.at[which], ag_send.at[0], ag_recv.at[which], tile, depth
        ).wait_recv()

    above = at(yrow + 1, zlo, core)
    below = at(yrow + 3, zlo, core)
    sibling = at(yrow, zlo, 1 - core)
    z_order = (1, 3, 2)
    pass_on(tile, above)
    pass_on(tile, below)
    for dz in z_order:
        pass_on(tile, at(yrow, zlo + dz, core))
    pass_on(tile, sibling)

    lax.fori_loop(4, 6, forward, 0)

    for dz in z_order:
        which = at(yrow, zlo + dz, core)
        arrived(which)
        pass_on(which, above)
        pass_on(which, below)
        pass_on(which, sibling)

    lax.fori_loop(6, 8, forward, 0)

    for dz in (0, 1, 3, 2):
        which = at(yrow + 3, zlo + dz, core)
        arrived(which)
        if dz in (0, 1):
            pass_on(which, above)
        pass_on(which, sibling)
        which = at(yrow + 1, zlo + dz, core)
        arrived(which)
        if dz in (2, 3):
            pass_on(which, below)
        pass_on(which, sibling)
    for dz in (0, 1, 3, 2):
        which = at(yrow + 2, zlo + dz, core)
        arrived(which)
        pass_on(which, sibling)
    for dy in range(4):
        for dz in range(4):
            arrived(at(yrow + dy, zlo + dz, 1 - core))

    def read_quads(ref, rows, rows2):
        return (
            ref[rows, pl.ds(0, HALF)],
            ref[rows, pl.ds(HALF, HALF)],
            ref[rows2, pl.ds(0, HALF)],
            ref[rows2, pl.ds(HALF, HALF)],
        )

    def rows_of(k):
        if isinstance(k, int):
            return pl.ds(8 * k, 8), pl.ds(HALF + 8 * k, 8)
        return pl.ds(pl.multiple_of(8 * k, 8), 8), pl.ds(pl.multiple_of(HALF + 8 * k, 8), 8)

    def table_of(p, k):
        which = k if p < 4 else 31 - k
        return tuple(table[which, p % 4, c] for c in range(4))

    def spectrum_block(t, k, first):
        rows, rows2 = rows_of(k)
        total = None
        for p in range(LOCAL_PLANES):
            hpr, hpi, hmr, hmi = table_of(p, k)
            pr, pi, mr, mi = quads_in(*read_quads(packed.at[t, p], rows, rows2), first)
            terms = times(hpr, hpi, pr, pi, first, False) + times(hmr, hmi, mr, mi, first, False)
            total = terms if total is None else tuple(a + b for a, b in zip(total, terms))
        cc, cs, sc, ss = quads_out(*total, first)
        sums[t, rows, pl.ds(0, HALF)] = cc
        sums[t, rows, pl.ds(HALF, HALF)] = cs
        sums[t, rows2, pl.ds(0, HALF)] = sc
        sums[t, rows2, pl.ds(HALF, HALF)] = ss

    for t in range(LOCAL_TILES):
        spectrum_block(t, 0, True)

        def later_blocks(k, carry, t=t):
            spectrum_block(t, k, False)
            return carry

        lax.fori_loop(1, 16, later_blocks, 0)
        half = dot3(split(sums[t]), inv_right())
        image[pl.ds(t * SIDE, SIDE), :] = dot3(inv_left(), split(half))

    rs_copies = []
    for s in range(SUBS):
        for d in (1, 3, 2):
            peer = lax.rem(xpos + d, 4)
            slot = (d - 1) * SUBS + s
            copy = remote(
                image.at[pl.ds(peer * 128 + s * SUB_ROWS, SUB_ROWS)],
                scattered.at[d - 1, pl.ds(s * SUB_ROWS, SUB_ROWS)],
                rs_send.at[slot],
                rs_recv.at[slot],
                tile,
                xpeer(d),
            )
            copy.start()
            rs_copies.append(copy)
    z_copies = []
    for s in range(SUBS):
        for copy in rs_copies[3 * s : 3 * s + 3]:
            copy.wait_recv()
        rows = pl.ds(s * SUB_ROWS, SUB_ROWS)
        own = image[pl.ds(xpos * 128 + s * SUB_ROWS, SUB_ROWS), :]
        zsend[rows, :] = own + scattered[0, rows, :] + scattered[1, rows, :] + scattered[2, rows, :]
        copy = remote(zsend.at[rows], zrecv.at[rows], z_send.at[s], z_recv.at[s], tile, zpartner)
        copy.start()
        z_copies.append(copy)
    local[1].wait()
    local[2].wait()
    xg_copies = []
    for s in range(SUBS):
        z_copies[s].wait_recv()
        rows = pl.ds(s * SUB_ROWS, SUB_ROWS)
        here = pl.ds(xpos * 128 + s * SUB_ROWS, SUB_ROWS)
        projection = background[here, :] + (zsend[rows, :] + zrecv[rows, :])
        ratio[here, :] = measured[here, :] / jnp.maximum(projection, FLOOR_LEVEL) - 1.0
        for d in (1, 3, 2):
            slot = (d - 1) * SUBS + s
            copy = remote(
                ratio.at[here], ratio.at[here], xg_send.at[slot], xg_recv.at[slot], tile, xpeer(d)
            )
            copy.start()
            xg_copies.append(copy)
    for copy in xg_copies:
        copy.wait_recv()

    for t in range(LOCAL_TILES):
        half = dot3(split(ratio[pl.ds(t * SIDE, SIDE), :]), right())
        sums[t] = dot3(left(), split(half))
        for k in range(16):
            rows, rows2 = rows_of(k)
            found = quads_in(*read_quads(sums.at[t], rows, rows2), k == 0)
            for c in range(4):
                ratio_quads[t, c, rows, :] = found[c]

    def strip(p, t, image_part, rows):
        values = vol[t, p, rows, :]
        return jnp.maximum(values * (1.0 + STEP_GAIN * image_part), 0.0)

    def send_halo(p):
        return (
            remote(
                top_send.at[p],
                after_recv.at[p],
                halo_send.at[p],
                halo_recv.at[p],
                before,
                depth,
            ),
            remote(
                bottom_send.at[p],
                before_recv.at[p],
                halo_send.at[LOCAL_PLANES + p],
                halo_recv.at[LOCAL_PLANES + p],
                after,
                depth,
            ),
        )

    def backward_plane(p, source):
        for t in range(LOCAL_TILES):
            for k in range(16):
                rows, rows2 = rows_of(k)
                hpr, hpi, hmr, hmi = (table[source(k), lax.rem(p, 4), c] for c in range(4))
                pr, pi, mr, mi = (ratio_quads[t, c, rows, :] for c in range(4))
                plus = times(hpr, hpi, pr, pi, k == 0, True)
                minus = times(hmr, hmi, mr, mi, k == 0, True)
                cc, cs, sc, ss = quads_out(*plus, *minus, k == 0)
                quads[t, rows, pl.ds(0, HALF)] = cc
                quads[t, rows, pl.ds(HALF, HALF)] = cs
                quads[t, rows2, pl.ds(0, HALF)] = sc
                quads[t, rows2, pl.ds(HALF, HALF)] = ss
            half = split(dot3(split(quads[t]), inv_right()))
            part_high[t, p] = half[0]
            part_low[t, p] = half[1]
            rows = slice(0, WIDTH) if t == 0 else slice(SIDE - WIDTH, SIDE)
            edge = strip(p, t, dot3((mats[4, rows], mats[5, rows]), half), rows)
            if t == 0:
                top_send[p] = edge
            else:
                bottom_send[p] = edge
        for copy in send_halo(p):
            copy.start()

    def backward_low(p, carry):
        backward_plane(p, lambda k: k)
        return carry

    def backward_high(p, carry):
        backward_plane(p, lambda k: 31 - k)
        return carry

    lax.fori_loop(0, 4, backward_low, 0)
    lax.fori_loop(4, 8, backward_high, 0)

    base = tile * LOCAL_TILES
    w_inner = ramp(margins[base])
    w_after = ramp(margins[base + 1])
    w_before = ramp(margins[lax.rem(base + TILES - 1, TILES)])

    def out_copies(p):
        return (
            pltpu.make_async_copy(
                vol.at[0, p, pl.ds(WIDTH, SIDE - WIDTH)],
                out_hbm.at[0, p, pl.ds(WIDTH, SIDE - WIDTH)],
                out_sem.at[2 * p],
            ),
            pltpu.make_async_copy(
                vol.at[1, p, pl.ds(0, SIDE - WIDTH)],
                out_hbm.at[1, p, pl.ds(0, SIDE - WIDTH)],
                out_sem.at[2 * p + 1],
            ),
        )

    def finish_plane(p, carry):
        half = (part_high[0, p], part_low[0, p])
        rows = slice(WIDTH, SIDE)
        upper = strip(p, 0, dot3((mats[4, rows], mats[5, rows]), half), rows)
        half = (part_high[1, p], part_low[1, p])
        rows = slice(0, SIDE - WIDTH)
        lower = strip(p, 1, dot3((mats[4, rows], mats[5, rows]), half), rows)
        inner = SIDE - 2 * WIDTH
        shared = (1.0 - w_inner) * upper[inner:] + w_inner * lower[:WIDTH]
        vol[0, p, WIDTH : SIDE - WIDTH, :] = upper[:inner]
        vol[0, p, SIDE - WIDTH :, :] = shared
        vol[1, p, :WIDTH, :] = shared
        vol[1, p, WIDTH : SIDE - WIDTH, :] = lower[WIDTH:]
        for copy in out_copies(p):
            copy.start()
        return carry

    lax.fori_loop(0, LOCAL_PLANES, finish_plane, 0)

    def outer_strips(p, carry):
        to_before, to_after = send_halo(p)
        to_before.wait_recv()
        to_after.wait_recv()
        vol[0, p, :WIDTH, :] = (1.0 - w_before) * before_recv[p] + w_before * top_send[p]
        vol[1, p, SIDE - WIDTH :, :] = (1.0 - w_after) * bottom_send[p] + w_after * after_recv[p]
        return carry

    lax.fori_loop(0, LOCAL_PLANES, outer_strips, 0)
    top_out = pltpu.make_async_copy(
        vol.at[0, :, pl.ds(0, WIDTH)], out_hbm.at[0, :, pl.ds(0, WIDTH)], out_sem.at[16]
    )
    bottom_out = pltpu.make_async_copy(
        vol.at[1, :, pl.ds(SIDE - WIDTH, WIDTH)],
        out_hbm.at[1, :, pl.ds(SIDE - WIDTH, WIDTH)],
        out_sem.at[17],
    )
    top_out.start()
    bottom_out.start()

    @pl.when(jnp.logical_not(negative))
    def _():
        up_all.wait_send()

    @pl.when(negative)
    def _():
        down_rest.wait_send()
        down_first.wait_send()
        down_last.wait_send()

    for copy in started + rs_copies + z_copies + xg_copies:
        copy.wait_send()

    def drain(p, carry):
        for copy in send_halo(p):
            copy.wait_send()
        for copy in out_copies(p):
            copy.wait()
        return carry

    lax.fori_loop(0, LOCAL_PLANES, drain, 0)
    top_out.wait()
    bottom_out.wait()


def on_device(volume, transfer, measured, background, margins, phases):
    mats = packed_tables()
    hbm = pl.BlockSpec(memory_space=pl.ANY)
    vmem = pl.BlockSpec(memory_space=pltpu.VMEM)
    smem = pl.BlockSpec(memory_space=pltpu.SMEM)
    dma = pltpu.SemaphoreType.DMA
    tall = LOCAL_TILES * SIDE
    return pl.pallas_call(
        kernel,
        name="update",
        out_shape=jax.ShapeDtypeStruct(volume.shape, f32),
        in_specs=[smem, smem, vmem, hbm, hbm, hbm, hbm, vmem],
        out_specs=hbm,
        scratch_shapes=[
            pltpu.VMEM((LOCAL_TILES, LOCAL_PLANES, SIDE, SIDE), f32),
            pltpu.VMEM((LOCAL_TILES, LOCAL_PLANES, SIDE, SIDE), f32),
            pltpu.VMEM((32, 4, 4, 8, HALF), f32),
            pltpu.VMEM((8, SIDE, SIDE), bf16),
            pltpu.VMEM((tall, SIDE), f32),
            pltpu.VMEM((tall, SIDE), f32),
            pltpu.VMEM((2, HALF, HALF), f32),
            pltpu.VMEM((2, 8, 16, HALF), f32),
            pltpu.VMEM((8, 16, HALF), f32),
            pltpu.VMEM((1, 16, HALF), f32),
            pltpu.VMEM((8, 16, HALF), f32),
            pltpu.VMEM((8, 16, HALF), f32),
            pltpu.VMEM((LOCAL_TILES, SIDE, SIDE), f32),
            pltpu.VMEM((tall, SIDE), f32),
            pltpu.VMEM((3, 128, SIDE), f32),
            pltpu.VMEM((128, SIDE), f32),
            pltpu.VMEM((128, SIDE), f32),
            pltpu.VMEM((tall, SIDE), f32),
            pltpu.VMEM((LOCAL_TILES, 4, HALF, HALF), f32),
            pltpu.VMEM((LOCAL_TILES, SIDE, SIDE), f32),
            pltpu.VMEM((LOCAL_TILES, LOCAL_PLANES, SIDE, SIDE), bf16),
            pltpu.VMEM((LOCAL_TILES, LOCAL_PLANES, SIDE, SIDE), bf16),
            pltpu.VMEM((LOCAL_PLANES, WIDTH, SIDE), f32),
            pltpu.VMEM((LOCAL_PLANES, WIDTH, SIDE), f32),
            pltpu.VMEM((LOCAL_PLANES, WIDTH, SIDE), f32),
            pltpu.VMEM((LOCAL_PLANES, WIDTH, SIDE), f32),
            dma((LOCAL_PLANES,)),
            dma((3,)),
            dma((3,)),
            dma((2,)),
            dma((31,)),
            dma((32,)),
            dma((3 * SUBS,)),
            dma((3 * SUBS,)),
            dma((SUBS,)),
            dma((SUBS,)),
            dma((3 * SUBS,)),
            dma((3 * SUBS,)),
            dma((2 * LOCAL_PLANES,)),
            dma((2 * LOCAL_PLANES,)),
            dma((2 * LOCAL_PLANES + 2,)),
        ],
        compiler_params=pltpu.CompilerParams(
            collective_id=0, has_side_effects=True, vmem_limit_bytes=40 * 1024 * 1024
        ),
    )(
        phases,
        margins,
        transfer,
        volume,
        measured.reshape(tall, SIDE),
        background.reshape(tall, SIDE),
        mats,
        pairing(),
    )


def solution(mesh):
    return jax.shard_map(
        on_device,
        mesh=mesh,
        in_specs=(
            P("tile", "depth", None, None),
            P("depth", None, "tile", None),
            P("tile", None, None),
            P("tile", None, None),
            P(),
            P("depth"),
        ),
        out_specs=P("tile", "depth", None, None),
        check_vma=False,
    )
```

time: 273 us -> 81.6 us (0.30)
  the two profiles are of different devices: /device:TPU:6 before, /device:TPU:8 now
where the time goes in v1:
time: 81.6 us; the launch traced here: 81.3 us
  Pallas kernels  70.8 us (87%)
  local copies, waits for them, and re-layouts  10.5 us (13%)
    pallas_call x1, Pallas kernels, on_device(): pl.pallas_call(kernel, name='update', out_shape=jax.ShapeDtypeStruct(volu...  70.8 us
    unnamed x17, local copies, waits for them, and re-layouts  10.5 us

profile of v1, /device:TPU:8, one launch (start us, length us, event | category | flops | bytes accessed | tf_op | source)
XLA Modules:
  0.0 81.3 jit_solution(16444168429615095731)
XLA Ops:
  0.0 0.0 copy-start
  0.0 2.2 %copy-done = f32[2,8,256,256]{3,2,1,0:T(8,128)S(1)} copy-done((f32[2,8,256,256]{3,2,1,0:T(8,128)S(1)}, f32[2,8,256,256]{3,2,1,0:T(8,128)}, u32[]{:S(2)}) %copy-start) | copy-done | bytes 4194328
  2.2 0.0 copy-start.1
  2.2 1.2 %copy-done.1 = bf16[8,256,256]{2,1,0:T(8,128)(2,1)S(1)} copy-done((bf16[8,256,256]{2,1,0:T(8,128)(2,1)S(1)}, bf16[8,256,256]{2,1,0:T(8,128)(2,1)}, u32[]{:S(2)}) %copy-start.1) | copy-done | bytes 1048600
  3.4 0.0 copy-start.2
  3.4 1.0 %copy-done.2 = f32[2,256,256]{2,1,0:T(8,128)S(1)} copy-done((f32[2,256,256]{2,1,0:T(8,128)S(1)}, f32[2,256,256]{2,1,0:T(8,128)}, u32[]{:S(2)}) %copy-start.2) | copy-done | bytes 524312
  4.5 0.0 copy-start.3
  4.5 1.0 %copy-done.3 = f32[2,256,256]{2,1,0:T(8,128)S(1)} copy-done((f32[2,256,256]{2,1,0:T(8,128)S(1)}, f32[2,256,256]{2,1,0:T(8,128)}, u32[]{:S(2)}) %copy-start.3) | copy-done | bytes 524312
  5.5 0.0 copy-start.4
  5.5 0.9 %copy-done.4 = f32[8,2,8,256]{3,2,1,0:T(8,128)S(1)} copy-done((f32[8,2,8,256]{3,2,1,0:T(8,128)S(1)}, f32[8,2,8,256]{3,2,1,0:T(8,128)}, u32[]{:S(2)}) %copy-start.4) | copy-done | bytes 131096
  6.4 0.0 copy-start.5
  6.4 0.8 copy-done.5
  7.2 0.0 copy-start.6
  7.2 0.7 copy-done.6
  7.8 0.0 copy-start.7
  7.8 0.7 copy-done.7
  8.5 70.8 %update.1 = f32[2,8,256,256]{3,2,1,0:T(8,128)S(1)} custom-call(s32[8]{0:T(128)S(1)} %copy-done.6, s32[64]{0:T(128)S(1)} %copy-done.7, f32[8,2,8,256]{3,2,1,0:T(8,128)S(1)} %copy-done.4, f32[2,8,256,256]{3,2,1,0:T(8,128)S(1)} %copy-done, f32[512,256]{1,0:T(8,128)S(1)} %bitcast.2, f32[512,256]{1,0:T(8,128)S(1)} %bitcast.3, bf16[8,256,256]{2,1,0:T(8,128)(2,1)S(1)} %copy-done.1, ...), custom_call_target="tpu_custom_call" | custom-call | tf_op jit(solution)/shard_map/update/pallas_call | solution.py:671
  79.3 2.0 %copy.10 = f32[2,8,256,256]{3,2,1,0:T(8,128)} copy(f32[2,8,256,256]{3,2,1,0:T(8,128)S(1)} %update.1) | data formatting | bytes 8388608
Async XLA Ops:
  0.0 2.2 %copy-start = (f32[2,8,256,256]{3,2,1,0:T(8,128)S(1)}, f32[2,8,256,256]{3,2,1,0:T(8,128)}, u32[]{:S(2)}) copy-start(f32[2,8,256,256]{3,2,1,0:T(8,128)} %volume_hbm.1) | copy-start | bytes 12582916
  2.2 1.2 %copy-start.1 = (bf16[8,256,256]{2,1,0:T(8,128)(2,1)S(1)}, bf16[8,256,256]{2,1,0:T(8,128)(2,1)}, u32[]{:S(2)}) copy-start(bf16[8,256,256]{2,1,0:T(8,128)(2,1)} %constant.4.clone.mats_hbm) | copy-start | bytes 3145732
  3.4 1.0 %copy-start.2 = (f32[2,256,256]{2,1,0:T(8,128)S(1)}, f32[2,256,256]{2,1,0:T(8,128)}, u32[]{:S(2)}) copy-start(f32[2,256,256]{2,1,0:T(8,128)} %param.10) | copy-start | bytes 1572868
  4.5 1.0 %copy-start.3 = (f32[2,256,256]{2,1,0:T(8,128)S(1)}, f32[2,256,256]{2,1,0:T(8,128)}, u32[]{:S(2)}) copy-start(f32[2,256,256]{2,1,0:T(8,128)} %param.11) | copy-start | bytes 1572868
  5.5 0.9 %copy-start.4 = (f32[8,2,8,256]{3,2,1,0:T(8,128)S(1)}, f32[8,2,8,256]{3,2,1,0:T(8,128)}, u32[]{:S(2)}) copy-start(f32[8,2,8,256]{3,2,1,0:T(8,128)} %transfer.1) | copy-start | bytes 393220
  6.4 0.8 copy-start.5
  7.2 0.7 copy-start.6
  7.8 0.7 copy-start.7

commit v2 on v1

--- a/solution.py
+++ b/solution.py
@@ -124,15 +124,19 @@
 
 
 def kernel(
-    phases,
-    margins,
-    transfer,
+    phases_hbm,
+    margins_hbm,
+    transfer_hbm,
     volume_hbm,
     measured_hbm,
     background_hbm,
     mats_hbm,
+    pair_hbm,
+    out_hbm,
+    phases,
+    margins,
+    transfer,
     pair_ref,
-    out_hbm,
     vol,
     packed,
     table,
@@ -204,8 +208,13 @@
         pltpu.make_async_copy(mats_hbm, mats, in_sem.at[0]),
         pltpu.make_async_copy(measured_hbm, measured, in_sem.at[1]),
         pltpu.make_async_copy(background_hbm, background, in_sem.at[2]),
+        pltpu.make_async_copy(transfer_hbm, transfer, in_sem.at[3]),
+        pltpu.make_async_copy(pair_hbm, pair_ref, in_sem.at[4]),
+        pltpu.make_async_copy(phases_hbm, phases, in_sem.at[5]),
+        pltpu.make_async_copy(margins_hbm, margins, in_sem.at[6]),
     ]
-    local[0].start()
+    for which in (3, 4, 0, 5, 6):
+        local[which].start()
     for copy in volume_copies:
         copy.start()
     local[1].start()
@@ -242,6 +251,8 @@
     def _():
         greet(row0_from, depth)
 
+    local[3].wait()
+    local[4].wait()
     whole = transfer[...].reshape(LOCAL_PLANES * 2 * 8, SIDE)
     halves[0] = whole[:, :HALF]
     rest = whole[:, HALF:]
@@ -320,6 +331,8 @@
         neg[0] = other0[0]
         neg[1:8] = mine[1, 1:8]
 
+    local[5].wait()
+    local[6].wait()
     plane0 = jnp.where(negative, 4, 0)
     column = lax.broadcasted_iota(jnp.int32, (4, HALF), 1)
     row4 = lax.broadcasted_iota(jnp.int32, (4, HALF), 0)
@@ -663,18 +676,20 @@
 
 def on_device(volume, transfer, measured, background, margins, phases):
     mats = packed_tables()
-    hbm = pl.BlockSpec(memory_space=pl.ANY)
-    vmem = pl.BlockSpec(memory_space=pltpu.VMEM)
-    smem = pl.BlockSpec(memory_space=pltpu.SMEM)
+    hbm = pl.BlockSpec(memory_space=pltpu.HBM)
     dma = pltpu.SemaphoreType.DMA
     tall = LOCAL_TILES * SIDE
     return pl.pallas_call(
         kernel,
         name="update",
         out_shape=jax.ShapeDtypeStruct(volume.shape, f32),
-        in_specs=[smem, smem, vmem, hbm, hbm, hbm, hbm, vmem],
-        out_specs=hbm,
+        in_specs=[hbm] * 8,
+        out_specs=pl.BlockSpec(memory_space=pl.ANY),
         scratch_shapes=[
+            pltpu.SMEM((LOCAL_PLANES,), jnp.int32),
+            pltpu.SMEM((TILES,), jnp.int32),
+            pltpu.VMEM((LOCAL_PLANES, 2, 8, SIDE), f32),
+            pltpu.VMEM((HALF, HALF), bf16),
             pltpu.VMEM((LOCAL_TILES, LOCAL_PLANES, SIDE, SIDE), f32),
             pltpu.VMEM((LOCAL_TILES, LOCAL_PLANES, SIDE, SIDE), f32),
             pltpu.VMEM((32, 4, 4, 8, HALF), f32),
@@ -702,7 +717,7 @@
             pltpu.VMEM((LOCAL_PLANES, WIDTH, SIDE), f32),
             pltpu.VMEM((LOCAL_PLANES, WIDTH, SIDE), f32),
             dma((LOCAL_PLANES,)),
-            dma((3,)),
+            dma((7,)),
             dma((3,)),
             dma((2,)),
             dma((31,)),
@@ -718,7 +733,7 @@
             dma((2 * LOCAL_PLANES + 2,)),
         ],
         compiler_params=pltpu.CompilerParams(
-            collective_id=0, has_side_effects=True, vmem_limit_bytes=40 * 1024 * 1024
+            collective_id=0, has_side_effects=True, vmem_limit_bytes=67043328
         ),
     )(
         phases,

time: 81.6 us -> 73 us (0.89)
  the two profiles are of different devices: /device:TPU:8 before, /device:TPU:6 now
where the time goes in v2:
time: 73 us; the launch traced here: 72.9 us
  Pallas kernels  68.3 us (94%)
  local copies, waits for them, and re-layouts  4.6 us (6%)
    pallas_call x1, Pallas kernels, on_device(): pl.pallas_call(kernel, name='update', out_shape=jax.ShapeDtypeStruct(volu...  68.3 us
    unnamed x1, local copies, waits for them, and re-layouts  4.6 us

profile of v2, /device:TPU:6, one launch (start us, length us, event | category | flops | bytes accessed | tf_op | source)
XLA Modules:
  0.0 72.9 jit_solution(1099079347971168241)
XLA Ops:
  0.0 68.3 %update.1 = f32[2,8,256,256]{3,2,1,0:T(8,128)} custom-call(s32[8]{0:T(128)} %phases_hbm.1, s32[64]{0:T(128)} %margins_hbm.1, f32[8,2,8,256]{3,2,1,0:T(8,128)} %transfer_hbm.1, f32[2,8,256,256]{3,2,1,0:T(8,128)} %volume_hbm.1, f32[512,256]{1,0:T(8,128)} %bitcast.2, f32[512,256]{1,0:T(8,128)} %bitcast.3, bf16[8,256,256]{2,1,0:T(8,128)(2,1)} %constant.4.clone.mats_hbm, ...), custom_call_target="tpu_custom_call" | custom-call | tf_op jit(solution)/shard_map/update/pallas_call | solution.py:682
  68.3 4.6 %copy.10 = f32[2,8,256,256]{3,2,1,0:T(8,128)} copy(f32[2,8,256,256]{3,2,1,0:T(8,128)} %update.1) | data formatting | bytes 8388608

commit v3 on v2

--- a/solution.py
+++ b/solution.py
@@ -15,7 +15,7 @@
 TILES = 64
 LOCAL_TILES = 2
 LOCAL_PLANES = 8
-SUBS = 2
+SUBS = 4
 SUB_ROWS = 128 // SUBS
 FLOOR_LEVEL = 0.5
 STEP_GAIN = 2.0
@@ -314,7 +314,7 @@
             packed[t, p] = dot3(left(), split(half))
         return carry
 
-    lax.fori_loop(0, 4, forward, 0)
+    lax.fori_loop(0, LOCAL_PLANES, forward, 0)
 
     @pl.when(jnp.logical_not(negative))
     def _():
@@ -406,16 +406,12 @@
         pass_on(tile, at(yrow, zlo + dz, core))
     pass_on(tile, sibling)
 
-    lax.fori_loop(4, 6, forward, 0)
-
     for dz in z_order:
         which = at(yrow, zlo + dz, core)
         arrived(which)
         pass_on(which, above)
         pass_on(which, below)
         pass_on(which, sibling)
-
-    lax.fori_loop(6, 8, forward, 0)
 
     for dz in (0, 1, 3, 2):
         which = at(yrow + 3, zlo + dz, core)
@@ -428,14 +424,6 @@
         if dz in (2, 3):
             pass_on(which, below)
         pass_on(which, sibling)
-    for dz in (0, 1, 3, 2):
-        which = at(yrow + 2, zlo + dz, core)
-        arrived(which)
-        pass_on(which, sibling)
-    for dy in range(4):
-        for dz in range(4):
-            arrived(at(yrow + dy, zlo + dz, 1 - core))
-
     def read_quads(ref, rows, rows2):
         return (
             ref[rows, pl.ds(0, HALF)],
@@ -467,38 +455,53 @@
         sums[t, rows2, pl.ds(0, HALF)] = sc
         sums[t, rows2, pl.ds(HALF, HALF)] = ss
 
+    def spectrum_group(t, start):
+        for j in range(1, 8):
+            spectrum_block(t, start + j, False)
+
+    near = 8 * jnp.where(jnp.logical_or(yrow == 0, yrow == 3), 0, 1)
+    far = 8 - near
+    for dy in (0, 1, 3):
+        for dz in range(4):
+            arrived(at(yrow + dy, zlo + dz, 1 - core))
+    spectrum_group(0, near)
+    for dz in (0, 1, 3, 2):
+        which = at(yrow + 2, zlo + dz, core)
+        arrived(which)
+        pass_on(which, sibling)
+    spectrum_group(1, near)
+    for dz in range(4):
+        arrived(at(yrow + 2, zlo + dz, 1 - core))
+
+    def rows_at(x, s):
+        return pl.ds((s // 2) * SIDE + x * 64 + (s % 2) * SUB_ROWS, SUB_ROWS)
+
+    rs_copies = []
     for t in range(LOCAL_TILES):
         spectrum_block(t, 0, True)
-
-        def later_blocks(k, carry, t=t):
-            spectrum_block(t, k, False)
-            return carry
-
-        lax.fori_loop(1, 16, later_blocks, 0)
+        spectrum_block(t, 8, False)
+        spectrum_group(t, far)
         half = dot3(split(sums[t]), inv_right())
         image[pl.ds(t * SIDE, SIDE), :] = dot3(inv_left(), split(half))
-
-    rs_copies = []
-    for s in range(SUBS):
-        for d in (1, 3, 2):
-            peer = lax.rem(xpos + d, 4)
-            slot = (d - 1) * SUBS + s
-            copy = remote(
-                image.at[pl.ds(peer * 128 + s * SUB_ROWS, SUB_ROWS)],
-                scattered.at[d - 1, pl.ds(s * SUB_ROWS, SUB_ROWS)],
-                rs_send.at[slot],
-                rs_recv.at[slot],
-                tile,
-                xpeer(d),
-            )
-            copy.start()
-            rs_copies.append(copy)
+        for s in (2 * t, 2 * t + 1):
+            for d in (1, 3, 2):
+                slot = (d - 1) * SUBS + s
+                copy = remote(
+                    image.at[rows_at(lax.rem(xpos + d, 4), s)],
+                    scattered.at[d - 1, pl.ds(s * SUB_ROWS, SUB_ROWS)],
+                    rs_send.at[slot],
+                    rs_recv.at[slot],
+                    tile,
+                    xpeer(d),
+                )
+                copy.start()
+                rs_copies.append(copy)
     z_copies = []
     for s in range(SUBS):
         for copy in rs_copies[3 * s : 3 * s + 3]:
             copy.wait_recv()
         rows = pl.ds(s * SUB_ROWS, SUB_ROWS)
-        own = image[pl.ds(xpos * 128 + s * SUB_ROWS, SUB_ROWS), :]
+        own = image[rows_at(xpos, s), :]
         zsend[rows, :] = own + scattered[0, rows, :] + scattered[1, rows, :] + scattered[2, rows, :]
         copy = remote(zsend.at[rows], zrecv.at[rows], z_send.at[s], z_recv.at[s], tile, zpartner)
         copy.start()
@@ -509,7 +512,7 @@
     for s in range(SUBS):
         z_copies[s].wait_recv()
         rows = pl.ds(s * SUB_ROWS, SUB_ROWS)
-        here = pl.ds(xpos * 128 + s * SUB_ROWS, SUB_ROWS)
+        here = rows_at(xpos, s)
         projection = background[here, :] + (zsend[rows, :] + zrecv[rows, :])
         ratio[here, :] = measured[here, :] / jnp.maximum(projection, FLOOR_LEVEL) - 1.0
         for d in (1, 3, 2):
@@ -519,10 +522,25 @@
             )
             copy.start()
             xg_copies.append(copy)
-    for copy in xg_copies:
-        copy.wait_recv()
+
+    def strip(p, t, image_part, rows):
+        values = vol[t, p, rows, :]
+        return jnp.maximum(values * (1.0 + STEP_GAIN * image_part), 0.0)
+
+    def to_before(p):
+        return remote(
+            top_send.at[p], after_recv.at[p], halo_send.at[p], halo_recv.at[p], before, depth
+        )
+
+    def to_after(p):
+        slot = LOCAL_PLANES + p
+        return remote(
+            bottom_send.at[p], before_recv.at[p], halo_send.at[slot], halo_recv.at[slot], after, depth
+        )
 
     for t in range(LOCAL_TILES):
+        for copy in xg_copies[6 * t : 6 * t + 6]:
+            copy.wait_recv()
         half = dot3(split(ratio[pl.ds(t * SIDE, SIDE), :]), right())
         sums[t] = dot3(left(), split(half))
         for k in range(16):
@@ -531,65 +549,35 @@
             for c in range(4):
                 ratio_quads[t, c, rows, :] = found[c]
 
-    def strip(p, t, image_part, rows):
-        values = vol[t, p, rows, :]
-        return jnp.maximum(values * (1.0 + STEP_GAIN * image_part), 0.0)
-
-    def send_halo(p):
-        return (
-            remote(
-                top_send.at[p],
-                after_recv.at[p],
-                halo_send.at[p],
-                halo_recv.at[p],
-                before,
-                depth,
-            ),
-            remote(
-                bottom_send.at[p],
-                before_recv.at[p],
-                halo_send.at[LOCAL_PLANES + p],
-                halo_recv.at[LOCAL_PLANES + p],
-                after,
-                depth,
-            ),
-        )
-
-    def backward_plane(p, source):
-        for t in range(LOCAL_TILES):
-            for k in range(16):
-                rows, rows2 = rows_of(k)
-                hpr, hpi, hmr, hmi = (table[source(k), lax.rem(p, 4), c] for c in range(4))
-                pr, pi, mr, mi = (ratio_quads[t, c, rows, :] for c in range(4))
-                plus = times(hpr, hpi, pr, pi, k == 0, True)
-                minus = times(hmr, hmi, mr, mi, k == 0, True)
-                cc, cs, sc, ss = quads_out(*plus, *minus, k == 0)
-                quads[t, rows, pl.ds(0, HALF)] = cc
-                quads[t, rows, pl.ds(HALF, HALF)] = cs
-                quads[t, rows2, pl.ds(0, HALF)] = sc
-                quads[t, rows2, pl.ds(HALF, HALF)] = ss
-            half = split(dot3(split(quads[t]), inv_right()))
-            part_high[t, p] = half[0]
-            part_low[t, p] = half[1]
-            rows = slice(0, WIDTH) if t == 0 else slice(SIDE - WIDTH, SIDE)
-            edge = strip(p, t, dot3((mats[4, rows], mats[5, rows]), half), rows)
-            if t == 0:
-                top_send[p] = edge
-            else:
-                bottom_send[p] = edge
-        for copy in send_halo(p):
-            copy.start()
-
-    def backward_low(p, carry):
-        backward_plane(p, lambda k: k)
-        return carry
-
-    def backward_high(p, carry):
-        backward_plane(p, lambda k: 31 - k)
-        return carry
-
-    lax.fori_loop(0, 4, backward_low, 0)
-    lax.fori_loop(4, 8, backward_high, 0)
+        def backward(q, carry, t=t):
+            for h in range(2):
+                p = q + 4 * h
+                for k in range(16):
+                    rows, rows2 = rows_of(k)
+                    which = 31 - k if h else k
+                    hpr, hpi, hmr, hmi = (table[which, q, c] for c in range(4))
+                    pr, pi, mr, mi = (ratio_quads[t, c, rows, :] for c in range(4))
+                    plus = times(hpr, hpi, pr, pi, k == 0, True)
+                    minus = times(hmr, hmi, mr, mi, k == 0, True)
+                    cc, cs, sc, ss = quads_out(*plus, *minus, k == 0)
+                    quads[h, rows, pl.ds(0, HALF)] = cc
+                    quads[h, rows, pl.ds(HALF, HALF)] = cs
+                    quads[h, rows2, pl.ds(0, HALF)] = sc
+                    quads[h, rows2, pl.ds(HALF, HALF)] = ss
+                half = split(dot3(split(quads[h]), inv_right()))
+                part_high[t, p] = half[0]
+                part_low[t, p] = half[1]
+                rows = slice(0, WIDTH) if t == 0 else slice(SIDE - WIDTH, SIDE)
+                edge = strip(p, t, dot3((mats[4, rows], mats[5, rows]), half), rows)
+                if t == 0:
+                    top_send[p] = edge
+                else:
+                    bottom_send[p] = edge
+            for h in range(2):
+                (to_after if t else to_before)(q + 4 * h).start()
+            return carry
+
+        lax.fori_loop(0, 4, backward, 0)
 
     base = tile * LOCAL_TILES
     w_inner = ramp(margins[base])
@@ -629,15 +617,6 @@
 
     lax.fori_loop(0, LOCAL_PLANES, finish_plane, 0)
 
-    def outer_strips(p, carry):
-        to_before, to_after = send_halo(p)
-        to_before.wait_recv()
-        to_after.wait_recv()
-        vol[0, p, :WIDTH, :] = (1.0 - w_before) * before_recv[p] + w_before * top_send[p]
-        vol[1, p, SIDE - WIDTH :, :] = (1.0 - w_after) * bottom_send[p] + w_after * after_recv[p]
-        return carry
-
-    lax.fori_loop(0, LOCAL_PLANES, outer_strips, 0)
     top_out = pltpu.make_async_copy(
         vol.at[0, :, pl.ds(0, WIDTH)], out_hbm.at[0, :, pl.ds(0, WIDTH)], out_sem.at[16]
     )
@@ -646,8 +625,22 @@
         out_hbm.at[1, :, pl.ds(SIDE - WIDTH, WIDTH)],
         out_sem.at[17],
     )
+
+    def last_strip(p, carry):
+        to_before(p).wait_recv()
+        vol[1, p, SIDE - WIDTH :, :] = (1.0 - w_after) * bottom_send[p] + w_after * after_recv[p]
+        return carry
+
+    lax.fori_loop(0, LOCAL_PLANES, last_strip, 0)
+    bottom_out.start()
+
+    def first_strip(p, carry):
+        to_after(p).wait_recv()
+        vol[0, p, :WIDTH, :] = (1.0 - w_before) * before_recv[p] + w_before * top_send[p]
+        return carry
+
+    lax.fori_loop(0, LOCAL_PLANES, first_strip, 0)
     top_out.start()
-    bottom_out.start()
 
     @pl.when(jnp.logical_not(negative))
     def _():
@@ -663,8 +656,8 @@
         copy.wait_send()
 
     def drain(p, carry):
-        for copy in send_halo(p):
-            copy.wait_send()
+        to_before(p).wait_send()
+        to_after(p).wait_send()
         for copy in out_copies(p):
             copy.wait()
         return carry

time: 73 us -> 68.6 us (0.940)
  Pallas kernels: 68.3 us -> 63.3 us
    pallas_call x1, Pallas kernels: 68.3 us -> 63.3 us  [on_device(): pl.pallas_call(kernel, name='update', out_shape=jax.ShapeDtypeStruct(volu...]
where the time goes in v3:
time: 68.6 us; the launch traced here: 67.9 us
  Pallas kernels  63.3 us (92%)
  local copies, waits for them, and re-layouts  4.6 us (7%)
    pallas_call x1, Pallas kernels, on_device(): pl.pallas_call(kernel, name='update', out_shape=jax.ShapeDtypeStruct(volu...  63.3 us
    unnamed x1, local copies, waits for them, and re-layouts  4.6 us

profile of v3, /device:TPU:6, one launch (start us, length us, event | category | flops | bytes accessed | tf_op | source)
XLA Modules:
  0.0 67.9 jit_solution(2642434723497401459)
XLA Ops:
  0.0 63.3 %update.1 = f32[2,8,256,256]{3,2,1,0:T(8,128)} custom-call(s32[8]{0:T(128)} %phases_hbm.1, s32[64]{0:T(128)} %margins_hbm.1, f32[8,2,8,256]{3,2,1,0:T(8,128)} %transfer_hbm.1, f32[2,8,256,256]{3,2,1,0:T(8,128)} %volume_hbm.1, f32[512,256]{1,0:T(8,128)} %bitcast.2, f32[512,256]{1,0:T(8,128)} %bitcast.3, bf16[8,256,256]{2,1,0:T(8,128)(2,1)} %constant.4.clone.mats_hbm, ...), custom_call_target="tpu_custom_call" | custom-call | tf_op jit(solution)/shard_map/update/pallas_call | solution.py:675
  63.3 4.6 %copy.10 = f32[2,8,256,256]{3,2,1,0:T(8,128)} copy(f32[2,8,256,256]{3,2,1,0:T(8,128)} %update.1) | data formatting | bytes 8388608

commit v4 on v3

--- a/solution.py
+++ b/solution.py
@@ -15,8 +15,7 @@
 TILES = 64
 LOCAL_TILES = 2
 LOCAL_PLANES = 8
-SUBS = 4
-SUB_ROWS = 128 // SUBS
+PIECES = 4
 FLOOR_LEVEL = 0.5
 STEP_GAIN = 2.0
 MESH = pl.DeviceIdType.MESH
@@ -150,11 +149,11 @@
     pos,
     neg,
     sums,
-    image,
+    partial,
     scattered,
     zsend,
     zrecv,
-    ratio,
+    spectrum,
     ratio_quads,
     quads,
     part_high,
@@ -441,7 +440,8 @@
         which = k if p < 4 else 31 - k
         return tuple(table[which, p % 4, c] for c in range(4))
 
-    def spectrum_block(t, k, first):
+    def spectrum_block(t, g, j, first):
+        k = 8 * g + j
         rows, rows2 = rows_of(k)
         total = None
         for p in range(LOCAL_PLANES):
@@ -450,17 +450,41 @@
             terms = times(hpr, hpi, pr, pi, first, False) + times(hmr, hmi, mr, mi, first, False)
             total = terms if total is None else tuple(a + b for a, b in zip(total, terms))
         cc, cs, sc, ss = quads_out(*total, first)
-        sums[t, rows, pl.ds(0, HALF)] = cc
-        sums[t, rows, pl.ds(HALF, HALF)] = cs
-        sums[t, rows2, pl.ds(0, HALF)] = sc
-        sums[t, rows2, pl.ds(HALF, HALF)] = ss
-
-    def spectrum_group(t, start):
+        upper, lower = pl.ds(8 * (j % 2), 8), pl.ds(16 + 8 * (j % 2), 8)
+        partial[t, g, j // 2, upper, pl.ds(0, HALF)] = cc
+        partial[t, g, j // 2, upper, pl.ds(HALF, HALF)] = cs
+        partial[t, g, j // 2, lower, pl.ds(0, HALF)] = sc
+        partial[t, g, j // 2, lower, pl.ds(HALF, HALF)] = ss
+
+    rs_copies = []
+
+    def spectrum_group(t, g):
         for j in range(1, 8):
-            spectrum_block(t, start + j, False)
-
-    near = 8 * jnp.where(jnp.logical_or(yrow == 0, yrow == 3), 0, 1)
-    far = 8 - near
+            spectrum_block(t, g, j, False)
+
+        @pl.when(g == 0)
+        def _():
+            spectrum_block(t, 0, 0, True)
+
+        @pl.when(g == 1)
+        def _():
+            spectrum_block(t, 1, 0, False)
+
+        s = len(rs_copies) // 3
+        for d in (1, 3, 2):
+            copy = remote(
+                partial.at[t, g, lax.rem(xpos + d, 4)],
+                scattered.at[d - 1, s],
+                rs_send.at[3 * s + d - 1],
+                rs_recv.at[3 * s + d - 1],
+                tile,
+                xpeer(d),
+            )
+            copy.start()
+            rs_copies.append(copy)
+
+    near = jnp.where(jnp.logical_or(yrow == 0, yrow == 3), 0, 1)
+    far = 1 - near
     for dy in (0, 1, 3):
         for dz in range(4):
             arrived(at(yrow + dy, zlo + dz, 1 - core))
@@ -472,53 +496,31 @@
     spectrum_group(1, near)
     for dz in range(4):
         arrived(at(yrow + 2, zlo + dz, 1 - core))
-
-    def rows_at(x, s):
-        return pl.ds((s // 2) * SIDE + x * 64 + (s % 2) * SUB_ROWS, SUB_ROWS)
-
-    rs_copies = []
-    for t in range(LOCAL_TILES):
-        spectrum_block(t, 0, True)
-        spectrum_block(t, 8, False)
-        spectrum_group(t, far)
-        half = dot3(split(sums[t]), inv_right())
-        image[pl.ds(t * SIDE, SIDE), :] = dot3(inv_left(), split(half))
-        for s in (2 * t, 2 * t + 1):
-            for d in (1, 3, 2):
-                slot = (d - 1) * SUBS + s
-                copy = remote(
-                    image.at[rows_at(lax.rem(xpos + d, 4), s)],
-                    scattered.at[d - 1, pl.ds(s * SUB_ROWS, SUB_ROWS)],
-                    rs_send.at[slot],
-                    rs_recv.at[slot],
-                    tile,
-                    xpeer(d),
-                )
-                copy.start()
-                rs_copies.append(copy)
+    spectrum_group(0, far)
+    spectrum_group(1, far)
+    pieces = ((0, near), (1, near), (0, far), (1, far))
     z_copies = []
-    for s in range(SUBS):
+    for s, (t, g) in enumerate(pieces):
         for copy in rs_copies[3 * s : 3 * s + 3]:
             copy.wait_recv()
-        rows = pl.ds(s * SUB_ROWS, SUB_ROWS)
-        own = image[rows_at(xpos, s), :]
-        zsend[rows, :] = own + scattered[0, rows, :] + scattered[1, rows, :] + scattered[2, rows, :]
-        copy = remote(zsend.at[rows], zrecv.at[rows], z_send.at[s], z_recv.at[s], tile, zpartner)
+        zsend[s] = partial[t, g, xpos] + scattered[0, s] + scattered[1, s] + scattered[2, s]
+        copy = remote(zsend.at[s], zrecv.at[s], z_send.at[s], z_recv.at[s], tile, zpartner)
         copy.start()
         z_copies.append(copy)
     local[1].wait()
     local[2].wait()
     xg_copies = []
-    for s in range(SUBS):
+    for s, (t, g) in enumerate(pieces):
         z_copies[s].wait_recv()
-        rows = pl.ds(s * SUB_ROWS, SUB_ROWS)
-        here = rows_at(xpos, s)
-        projection = background[here, :] + (zsend[rows, :] + zrecv[rows, :])
-        ratio[here, :] = measured[here, :] / jnp.maximum(projection, FLOOR_LEVEL) - 1.0
+        spectrum[t, g, xpos] = zsend[s] + zrecv[s]
         for d in (1, 3, 2):
-            slot = (d - 1) * SUBS + s
             copy = remote(
-                ratio.at[here], ratio.at[here], xg_send.at[slot], xg_recv.at[slot], tile, xpeer(d)
+                spectrum.at[t, g, xpos],
+                spectrum.at[t, g, xpos],
+                xg_send.at[3 * s + d - 1],
+                xg_recv.at[3 * s + d - 1],
+                tile,
+                xpeer(d),
             )
             copy.start()
             xg_copies.append(copy)
@@ -539,9 +541,18 @@
         )
 
     for t in range(LOCAL_TILES):
-        for copy in xg_copies[6 * t : 6 * t + 6]:
+        for copy in xg_copies[3 * t : 3 * t + 3] + xg_copies[3 * t + 6 : 3 * t + 9]:
             copy.wait_recv()
-        half = dot3(split(ratio[pl.ds(t * SIDE, SIDE), :]), right())
+        for k in range(16):
+            rows, rows2 = rows_of(k)
+            found = spectrum.at[t, k // 8, (k % 8) // 2]
+            sums[t, rows, :] = found[pl.ds(8 * (k % 2), 8), :]
+            sums[t, rows2, :] = found[pl.ds(16 + 8 * (k % 2), 8), :]
+        half = dot3(split(sums[t]), inv_right())
+        here = pl.ds(t * SIDE, SIDE)
+        projection = background[here, :] + dot3(inv_left(), split(half))
+        ratio = measured[here, :] / jnp.maximum(projection, FLOOR_LEVEL)
+        half = dot3(split(ratio - 1.0), right())
         sums[t] = dot3(left(), split(half))
         for k in range(16):
             rows, rows2 = rows_of(k)
@@ -696,11 +707,11 @@
             pltpu.VMEM((8, 16, HALF), f32),
             pltpu.VMEM((8, 16, HALF), f32),
             pltpu.VMEM((LOCAL_TILES, SIDE, SIDE), f32),
-            pltpu.VMEM((tall, SIDE), f32),
-            pltpu.VMEM((3, 128, SIDE), f32),
-            pltpu.VMEM((128, SIDE), f32),
-            pltpu.VMEM((128, SIDE), f32),
-            pltpu.VMEM((tall, SIDE), f32),
+            pltpu.VMEM((LOCAL_TILES, 2, 4, WIDTH, SIDE), f32),
+            pltpu.VMEM((3, PIECES, WIDTH, SIDE), f32),
+            pltpu.VMEM((PIECES, WIDTH, SIDE), f32),
+            pltpu.VMEM((PIECES, WIDTH, SIDE), f32),
+            pltpu.VMEM((LOCAL_TILES, 2, 4, WIDTH, SIDE), f32),
             pltpu.VMEM((LOCAL_TILES, 4, HALF, HALF), f32),
             pltpu.VMEM((LOCAL_TILES, SIDE, SIDE), f32),
             pltpu.VMEM((LOCAL_TILES, LOCAL_PLANES, SIDE, SIDE), bf16),
@@ -715,28 +726,33 @@
             dma((2,)),
             dma((31,)),
             dma((32,)),
-            dma((3 * SUBS,)),
-            dma((3 * SUBS,)),
-            dma((SUBS,)),
-            dma((SUBS,)),
-            dma((3 * SUBS,)),
-            dma((3 * SUBS,)),
+            dma((3 * PIECES,)),
+            dma((3 * PIECES,)),
+            dma((PIECES,)),
+            dma((PIECES,)),
+            dma((3 * PIECES,)),
+            dma((3 * PIECES,)),
             dma((2 * LOCAL_PLANES,)),
             dma((2 * LOCAL_PLANES,)),
             dma((2 * LOCAL_PLANES + 2,)),
         ],
         compiler_params=pltpu.CompilerParams(
-            collective_id=0, has_side_effects=True, vmem_limit_bytes=67043328
+            collective_id=0, has_side_effects=True, vmem_limit_bytes=48 * 1024 * 1024
         ),
     )(
-        phases,
-        margins,
-        transfer,
-        volume,
-        measured.reshape(tall, SIDE),
-        background.reshape(tall, SIDE),
-        mats,
-        pairing(),
+        *(
+            pltpu.with_memory_space_constraint(array, pltpu.HBM)
+            for array in (
+                phases,
+                margins,
+                transfer,
+                volume,
+                measured.reshape(tall, SIDE),
+                background.reshape(tall, SIDE),
+                mats,
+                pairing(),
+            )
+        )
     )
 
 

time: 68.6 us -> 68.9 us (level)
  Pallas kernels: 63.3 us -> 66.5 us
  local copies, waits for them, and re-layouts: 4.6 us -> 2.02 us
    pallas_call x1, Pallas kernels: 63.3 us -> 66.5 us  [on_device(): pl.pallas_call(kernel, name='update', out_shape=jax.ShapeDtypeStruct(volu...]
    unnamed x1, local copies, waits for them, and re-layouts: 4.6 us -> 2.02 us
where the time goes in v4:
time: 68.9 us; the launch traced here: 68.5 us
  Pallas kernels  66.5 us (97%)
  local copies, waits for them, and re-layouts  2.02 us (3%)
    pallas_call x1, Pallas kernels, on_device(): pl.pallas_call(kernel, name='update', out_shape=jax.ShapeDtypeStruct(volu...  66.5 us
    unnamed x1, local copies, waits for them, and re-layouts  2.02 us

profile of v4, /device:TPU:6, one launch (start us, length us, event | category | flops | bytes accessed | tf_op | source)
XLA Modules:
  0.0 68.5 jit_solution(98433756116079176)
XLA Ops:
  0.0 66.5 %update.1 = f32[2,8,256,256]{3,2,1,0:T(8,128)S(1)} custom-call(s32[8]{0:T(128)} %phases_hbm.1, s32[64]{0:T(128)} %margins_hbm.1, f32[8,2,8,256]{3,2,1,0:T(8,128)} %transfer_hbm.1, f32[2,8,256,256]{3,2,1,0:T(8,128)} %volume_hbm.1, f32[512,256]{1,0:T(8,128)} %bitcast.2, f32[512,256]{1,0:T(8,128)} %bitcast.3, bf16[8,256,256]{2,1,0:T(8,128)(2,1)} %constant.4.clone.mats_hbm, ...), custom_call_target="tpu_custom_call" | custom-call | tf_op jit(solution)/shard_map/update/pallas_call | solution.py:686
  66.5 2.0 %copy.10 = f32[2,8,256,256]{3,2,1,0:T(8,128)} copy(f32[2,8,256,256]{3,2,1,0:T(8,128)S(1)} %update.1) | data formatting | bytes 8388608

commit v5 on v4

--- a/solution.py
+++ b/solution.py
@@ -131,7 +131,7 @@
     background_hbm,
     mats_hbm,
     pair_hbm,
-    out_hbm,
+    out,
     phases,
     margins,
     transfer,
@@ -176,7 +176,6 @@
     xg_recv,
     halo_send,
     halo_recv,
-    out_sem,
 ):
     tile = lax.axis_index("tile")
     depth = lax.axis_index("depth")
@@ -595,20 +594,6 @@
     w_after = ramp(margins[base + 1])
     w_before = ramp(margins[lax.rem(base + TILES - 1, TILES)])
 
-    def out_copies(p):
-        return (
-            pltpu.make_async_copy(
-                vol.at[0, p, pl.ds(WIDTH, SIDE - WIDTH)],
-                out_hbm.at[0, p, pl.ds(WIDTH, SIDE - WIDTH)],
-                out_sem.at[2 * p],
-            ),
-            pltpu.make_async_copy(
-                vol.at[1, p, pl.ds(0, SIDE - WIDTH)],
-                out_hbm.at[1, p, pl.ds(0, SIDE - WIDTH)],
-                out_sem.at[2 * p + 1],
-            ),
-        )
-
     def finish_plane(p, carry):
         half = (part_high[0, p], part_low[0, p])
         rows = slice(WIDTH, SIDE)
@@ -618,40 +603,27 @@
         lower = strip(p, 1, dot3((mats[4, rows], mats[5, rows]), half), rows)
         inner = SIDE - 2 * WIDTH
         shared = (1.0 - w_inner) * upper[inner:] + w_inner * lower[:WIDTH]
-        vol[0, p, WIDTH : SIDE - WIDTH, :] = upper[:inner]
-        vol[0, p, SIDE - WIDTH :, :] = shared
-        vol[1, p, :WIDTH, :] = shared
-        vol[1, p, WIDTH : SIDE - WIDTH, :] = lower[WIDTH:]
-        for copy in out_copies(p):
-            copy.start()
+        out[0, p, WIDTH : SIDE - WIDTH, :] = upper[:inner]
+        out[0, p, SIDE - WIDTH :, :] = shared
+        out[1, p, :WIDTH, :] = shared
+        out[1, p, WIDTH : SIDE - WIDTH, :] = lower[WIDTH:]
         return carry
 
     lax.fori_loop(0, LOCAL_PLANES, finish_plane, 0)
-
-    top_out = pltpu.make_async_copy(
-        vol.at[0, :, pl.ds(0, WIDTH)], out_hbm.at[0, :, pl.ds(0, WIDTH)], out_sem.at[16]
-    )
-    bottom_out = pltpu.make_async_copy(
-        vol.at[1, :, pl.ds(SIDE - WIDTH, WIDTH)],
-        out_hbm.at[1, :, pl.ds(SIDE - WIDTH, WIDTH)],
-        out_sem.at[17],
-    )
 
     def last_strip(p, carry):
         to_before(p).wait_recv()
-        vol[1, p, SIDE - WIDTH :, :] = (1.0 - w_after) * bottom_send[p] + w_after * after_recv[p]
+        out[1, p, SIDE - WIDTH :, :] = (1.0 - w_after) * bottom_send[p] + w_after * after_recv[p]
         return carry
 
     lax.fori_loop(0, LOCAL_PLANES, last_strip, 0)
-    bottom_out.start()
 
     def first_strip(p, carry):
         to_after(p).wait_recv()
-        vol[0, p, :WIDTH, :] = (1.0 - w_before) * before_recv[p] + w_before * top_send[p]
+        out[0, p, :WIDTH, :] = (1.0 - w_before) * before_recv[p] + w_before * top_send[p]
         return carry
 
     lax.fori_loop(0, LOCAL_PLANES, first_strip, 0)
-    top_out.start()
 
     @pl.when(jnp.logical_not(negative))
     def _():
@@ -669,13 +641,9 @@
     def drain(p, carry):
         to_before(p).wait_send()
         to_after(p).wait_send()
-        for copy in out_copies(p):
-            copy.wait()
         return carry
 
     lax.fori_loop(0, LOCAL_PLANES, drain, 0)
-    top_out.wait()
-    bottom_out.wait()
 
 
 def on_device(volume, transfer, measured, background, margins, phases):
@@ -688,7 +656,7 @@
         name="update",
         out_shape=jax.ShapeDtypeStruct(volume.shape, f32),
         in_specs=[hbm] * 8,
-        out_specs=pl.BlockSpec(memory_space=pl.ANY),
+        out_specs=pl.BlockSpec(memory_space=pltpu.VMEM),
         scratch_shapes=[
             pltpu.SMEM((LOCAL_PLANES,), jnp.int32),
             pltpu.SMEM((TILES,), jnp.int32),
@@ -734,7 +702,6 @@
             dma((3 * PIECES,)),
             dma((2 * LOCAL_PLANES,)),
             dma((2 * LOCAL_PLANES,)),
-            dma((2 * LOCAL_PLANES + 2,)),
         ],
         compiler_params=pltpu.CompilerParams(
             collective_id=0, has_side_effects=True, vmem_limit_bytes=48 * 1024 * 1024

time: 68.9 us -> 64.1 us (0.930)
  Pallas kernels: 66.5 us -> 62 us
    pallas_call x1, Pallas kernels: 66.5 us -> 62 us  [on_device(): pl.pallas_call(kernel, name='update', out_shape=jax.ShapeDtypeStruct(volu...]
where the time goes in v5:
time: 64.1 us; the launch traced here: 64 us
  Pallas kernels  62 us (97%)
  local copies, waits for them, and re-layouts  2.02 us (3%)
    pallas_call x1, Pallas kernels, on_device(): pl.pallas_call(kernel, name='update', out_shape=jax.ShapeDtypeStruct(volu...  62 us
    unnamed x1, local copies, waits for them, and re-layouts  2.02 us

profile of v5, /device:TPU:6, one launch (start us, length us, event | category | flops | bytes accessed | tf_op | source)
XLA Modules:
  0.0 64.0 jit_solution(17620276651531565099)
XLA Ops:
  0.0 62.0 %update.1 = f32[2,8,256,256]{3,2,1,0:T(8,128)S(1)} custom-call(s32[8]{0:T(128)} %phases_hbm.1, s32[64]{0:T(128)} %margins_hbm.1, f32[8,2,8,256]{3,2,1,0:T(8,128)} %transfer_hbm.1, f32[2,8,256,256]{3,2,1,0:T(8,128)} %volume_hbm.1, f32[512,256]{1,0:T(8,128)} %bitcast.2, f32[512,256]{1,0:T(8,128)} %bitcast.3, bf16[8,256,256]{2,1,0:T(8,128)(2,1)} %constant.4.clone.mats_hbm, ...), custom_call_target="tpu_custom_call" | custom-call | tf_op jit(solution)/shard_map/update/pallas_call | solution.py:654
  62.0 2.0 %copy.10 = f32[2,8,256,256]{3,2,1,0:T(8,128)} copy(f32[2,8,256,256]{3,2,1,0:T(8,128)S(1)} %update.1) | data formatting | bytes 8388608

commit v6 on v5

--- a/solution.py
+++ b/solution.py
@@ -16,6 +16,7 @@
 LOCAL_TILES = 2
 LOCAL_PLANES = 8
 PIECES = 4
+GATHER_SENDS = 62
 FLOOR_LEVEL = 0.5
 STEP_GAIN = 2.0
 MESH = pl.DeviceIdType.MESH
@@ -228,6 +229,7 @@
         greet(at(yrow, zlo + dz, core), depth)
     greet(at(yrow + 1, zlo, core), depth)
     greet(at(yrow + 3, zlo, core), depth)
+    greet(at(yrow + 2, zlo, core), depth)
     greet(at(yrow, zlo, 1 - core), depth)
     for d in range(1, 4):
         greet(tile, xpeer(d))
@@ -260,13 +262,13 @@
     halves[1] = dot(high, move) + dot(low, move) + dot(lowest, move)
     for r in range(8):
         to = jnp.where(negative, (8 - r) % 8, r)
-        for ph in range(2):
+        for n in range(4):
             for e in range(2):
                 for c in range(2):
-                    piece = halves[e, pl.ds(ph * 64 + c * 8 + r, 4, stride=16), :]
-                    mine[ph, to, pl.ds((e * 2 + c) * 4, 4), :] = piece
-
-    pl.semaphore_wait(barrier, 14 + 2 * (tile // 16))
+                    piece = halves[e, pl.ds(n * 32 + c * 8 + r, 2, stride=16), :]
+                    mine[n // 2, n % 2, to, pl.ds((e * 2 + c) * 2, 2), :] = piece
+
+    pl.semaphore_wait(barrier, 15 + 2 * (tile // 16))
 
     def remote(src, dst, send, recv, t, d):
         return pltpu.make_async_remote_copy(
@@ -280,24 +282,31 @@
 
     rows7 = pl.ds(1, 7)
     row1 = pl.ds(0, 1)
-    up_all = remote(mine.at[1], other, ex_send.at[0], ex_recv.at[0], 31 - tile, depth)
-    down_rest = remote(
-        mine.at[0, rows7], other.at[rows7], ex_send.at[0], ex_recv.at[0], 31 - tile, depth
-    )
-    down_first = remote(
-        mine.at[0, row1], other.at[row1], ex_send.at[1], ex_recv.at[1], first_of, depth
-    )
-    down_last = remote(mine.at[1, row1], other0, ex_send.at[2], ex_recv.at[1], last_to, depth)
+
+    def exchange(n):
+        send = lambda k: ex_send.at[3 * n + k]
+        recv = lambda k: ex_recv.at[2 * n + k]
+        return (
+            remote(mine.at[1, n], other.at[n], send(0), recv(0), 31 - tile, depth),
+            remote(
+                mine.at[0, n, rows7], other.at[n, rows7], send(0), recv(0), 31 - tile, depth
+            ),
+            remote(mine.at[0, n, row1], other.at[n, row1], send(1), recv(1), first_of, depth),
+            remote(mine.at[1, n, row1], other0.at[n], send(2), recv(1), last_to, depth),
+        )
+
+    exchanges = (exchange(0), exchange(1))
 
     @pl.when(jnp.logical_not(negative))
     def _():
-        up_all.start()
+        for n in range(2):
+            exchanges[n][0].start()
 
     @pl.when(negative)
     def _():
-        down_rest.start()
-        down_first.start()
-        down_last.start()
+        for n in range(2):
+            for copy in exchanges[n][1:]:
+                copy.start()
 
     left = lambda: (mats[0], mats[1])
     right = lambda: (mats[2], mats[3])
@@ -314,114 +323,128 @@
 
     lax.fori_loop(0, LOCAL_PLANES, forward, 0)
 
-    @pl.when(jnp.logical_not(negative))
-    def _():
-        down_rest.wait_recv()
-        down_first.wait_recv()
-        pos[...] = mine[0]
-        neg[...] = other[...]
-
-    @pl.when(negative)
-    def _():
-        up_all.wait_recv()
-        down_last.wait_recv()
-        pos[...] = other[...]
-        neg[0] = other0[0]
-        neg[1:8] = mine[1, 1:8]
+    started = []
+
+    def pass_on(which, n, t):
+        copy = remote(
+            table.at[which, pl.ds(2 * n, 2)],
+            table.at[which, pl.ds(2 * n, 2)],
+            ag_send.at[len(started)],
+            ag_recv.at[2 * which + n],
+            t,
+            depth,
+        )
+        copy.start()
+        started.append(copy)
+
+    def arrived(which, n):
+        remote(
+            table.at[which, pl.ds(2 * n, 2)],
+            table.at[which, pl.ds(2 * n, 2)],
+            ag_send.at[0],
+            ag_recv.at[2 * which + n],
+            tile,
+            depth,
+        ).wait_recv()
+
+    above = at(yrow + 1, zlo, core)
+    below = at(yrow + 3, zlo, core)
+    across = at(yrow + 2, zlo, core)
+    sibling = at(yrow, zlo, 1 - core)
+    z_order = (1, 3, 2)
 
     local[5].wait()
     local[6].wait()
     plane0 = jnp.where(negative, 4, 0)
-    column = lax.broadcasted_iota(jnp.int32, (4, HALF), 1)
-    row4 = lax.broadcasted_iota(jnp.int32, (4, HALF), 0)
-    phase = jnp.zeros((4, HALF), jnp.int32)
-    for q in range(4):
-        phase = jnp.where(row4 == q, phases[plane0 + q], phase)
+    column = lax.broadcasted_iota(jnp.int32, (2, HALF), 1)
+    row2 = lax.broadcasted_iota(jnp.int32, (2, HALF), 0)
     lane0 = column == 0
-
-    def rotor(columns):
-        angle = ((phase * columns) & (SIDE - 1)).astype(f32) * (2.0 * math.pi / SIDE)
-        return jnp.cos(angle), jnp.sin(angle)
-
-    cos_p, sin_p = rotor(column)
-    cos_m, sin_m = rotor(jnp.where(lane0, HALF, column))
-    sin_m = jnp.where(lane0, 0.0, sin_m)
     is_first = block == 0
-    for r in range(8):
-        epr, epi, fpr, fpi = (pos[r, pl.ds(c * 4, 4), :] for c in range(4))
-        enr, eni, fnr, fni = (neg[r, pl.ds(c * 4, 4), :] for c in range(4))
-        hpr, hpi = 0.25 * (epr + fnr), 0.25 * (epi - fni)
-        hmr, hmi = 0.25 * (enr + fpr), 0.25 * (eni - fpi)
-        if r == 0:
-            at0 = jnp.logical_and(is_first, jnp.logical_not(lane0))
-            hpr = jnp.where(at0, 0.5 * (epr + fpr), hpr)
-            hpi = jnp.where(at0, 0.5 * (epi - fpi), hpi)
-            hmr = jnp.where(at0, 0.5 * (enr + fnr), hmr)
-            hmi = jnp.where(at0, 0.5 * (eni - fni), hmi)
-        lpr, lpi = 0.5 * (epr + enr), 0.5 * (epi - eni)
-        lmr, lmi = 0.5 * (fpr + fnr), 0.5 * (fpi - fni)
-        if r == 0:
-            lpr, lpi = jnp.where(is_first, epr, lpr), jnp.where(is_first, enr, lpi)
-            lmr, lmi = jnp.where(is_first, fpr, lmr), jnp.where(is_first, fnr, lmi)
-        hpr, hpi = jnp.where(lane0, lpr, hpr), jnp.where(lane0, lpi, hpi)
-        hmr, hmi = jnp.where(lane0, lmr, hmr), jnp.where(lane0, lmi, hmi)
-        parts = (
-            hpr * cos_p + hpi * sin_p,
-            hpi * cos_p - hpr * sin_p,
-            hmr * cos_m + hmi * sin_m,
-            hmi * cos_m - hmr * sin_m,
-        )
-        for c in range(4):
-            for q in range(4):
-                table[tile, q, c, pl.ds(r, 1), :] = parts[c][q : q + 1]
-
-    started = []
-
-    def pass_on(which, t):
-        copy = remote(
-            table.at[which],
-            table.at[which],
-            ag_send.at[len(started)],
-            ag_recv.at[which],
-            t,
-            depth,
-        )
-        copy.start()
-        started.append(copy)
-
-    def arrived(which):
-        remote(
-            table.at[which], table.at[which], ag_send.at[0], ag_recv.at[which], tile, depth
-        ).wait_recv()
-
-    above = at(yrow + 1, zlo, core)
-    below = at(yrow + 3, zlo, core)
-    sibling = at(yrow, zlo, 1 - core)
-    z_order = (1, 3, 2)
-    pass_on(tile, above)
-    pass_on(tile, below)
-    for dz in z_order:
-        pass_on(tile, at(yrow, zlo + dz, core))
-    pass_on(tile, sibling)
-
-    for dz in z_order:
-        which = at(yrow, zlo + dz, core)
-        arrived(which)
-        pass_on(which, above)
-        pass_on(which, below)
-        pass_on(which, sibling)
-
-    for dz in (0, 1, 3, 2):
+    for n in range(2):
+
+        @pl.when(jnp.logical_not(negative))
+        def _(n=n):
+            exchanges[n][1].wait_recv()
+            exchanges[n][2].wait_recv()
+            pos[n] = mine[0, n]
+            neg[n] = other[n]
+
+        @pl.when(negative)
+        def _(n=n):
+            exchanges[n][0].wait_recv()
+            exchanges[n][3].wait_recv()
+            pos[n] = other[n]
+            neg[n, 0] = other0[n, 0]
+            neg[n, 1:8] = mine[1, n, 1:8]
+
+        phase = jnp.where(row2 == 0, phases[plane0 + 2 * n], phases[plane0 + 2 * n + 1])
+
+        def rotor(columns):
+            angle = ((phase * columns) & (SIDE - 1)).astype(f32) * (2.0 * math.pi / SIDE)
+            return jnp.cos(angle), jnp.sin(angle)
+
+        cos_p, sin_p = rotor(column)
+        cos_m, sin_m = rotor(jnp.where(lane0, HALF, column))
+        sin_m = jnp.where(lane0, 0.0, sin_m)
+        for r in range(8):
+            epr, epi, fpr, fpi = (pos[n, r, pl.ds(c * 2, 2), :] for c in range(4))
+            enr, eni, fnr, fni = (neg[n, r, pl.ds(c * 2, 2), :] for c in range(4))
+            hpr, hpi = 0.25 * (epr + fnr), 0.25 * (epi - fni)
+            hmr, hmi = 0.25 * (enr + fpr), 0.25 * (eni - fpi)
+            if r == 0:
+                at0 = jnp.logical_and(is_first, jnp.logical_not(lane0))
+                hpr = jnp.where(at0, 0.5 * (epr + fpr), hpr)
+                hpi = jnp.where(at0, 0.5 * (epi - fpi), hpi)
+                hmr = jnp.where(at0, 0.5 * (enr + fnr), hmr)
+                hmi = jnp.where(at0, 0.5 * (eni - fni), hmi)
+            lpr, lpi = 0.5 * (epr + enr), 0.5 * (epi - eni)
+            lmr, lmi = 0.5 * (fpr + fnr), 0.5 * (fpi - fni)
+            if r == 0:
+                lpr, lpi = jnp.where(is_first, epr, lpr), jnp.where(is_first, enr, lpi)
+                lmr, lmi = jnp.where(is_first, fpr, lmr), jnp.where(is_first, fnr, lmi)
+            hpr, hpi = jnp.where(lane0, lpr, hpr), jnp.where(lane0, lpi, hpi)
+            hmr, hmi = jnp.where(lane0, lmr, hmr), jnp.where(lane0, lmi, hmi)
+            parts = (
+                hpr * cos_p + hpi * sin_p,
+                hpi * cos_p - hpr * sin_p,
+                hmr * cos_m + hmi * sin_m,
+                hmi * cos_m - hmr * sin_m,
+            )
+            for c in range(4):
+                for q in range(2):
+                    table[tile, 2 * n + q, c, pl.ds(r, 1), :] = parts[c][q : q + 1]
+        for dz in z_order:
+            pass_on(tile, n, at(yrow, zlo + dz, core))
+        pass_on(tile, n, above)
+        pass_on(tile, n, below)
+        pass_on(tile, n, sibling)
+
+    def relay(dz, n):
         which = at(yrow + 3, zlo + dz, core)
-        arrived(which)
+        arrived(which, n)
         if dz in (0, 1):
-            pass_on(which, above)
-        pass_on(which, sibling)
+            pass_on(which, n, above)
+        pass_on(which, n, sibling)
         which = at(yrow + 1, zlo + dz, core)
-        arrived(which)
-        if dz in (2, 3):
-            pass_on(which, below)
-        pass_on(which, sibling)
+        arrived(which, n)
+        if dz == 3:
+            pass_on(which, n, below)
+        pass_on(which, n, sibling)
+
+    for n in range(2):
+        for dz in z_order:
+            which = at(yrow, zlo + dz, core)
+            arrived(which, n)
+            if dz == 2:
+                pass_on(which, n, across)
+            pass_on(which, n, above)
+            pass_on(which, n, below)
+            pass_on(which, n, sibling)
+        relay(0, n)
+    for n in range(2):
+        for dz in z_order:
+            relay(dz, n)
+
     def read_quads(ref, rows, rows2):
         return (
             ref[rows, pl.ds(0, HALF)],
@@ -486,15 +509,18 @@
     far = 1 - near
     for dy in (0, 1, 3):
         for dz in range(4):
-            arrived(at(yrow + dy, zlo + dz, 1 - core))
+            for n in range(2):
+                arrived(at(yrow + dy, zlo + dz, 1 - core), n)
     spectrum_group(0, near)
-    for dz in (0, 1, 3, 2):
-        which = at(yrow + 2, zlo + dz, core)
-        arrived(which)
-        pass_on(which, sibling)
+    for n in range(2):
+        for dz in (0, 1, 3, 2):
+            which = at(yrow + 2, zlo + dz, core)
+            arrived(which, n)
+            pass_on(which, n, sibling)
     spectrum_group(1, near)
     for dz in range(4):
-        arrived(at(yrow + 2, zlo + dz, 1 - core))
+        for n in range(2):
+            arrived(at(yrow + 2, zlo + dz, 1 - core), n)
     spectrum_group(0, far)
     spectrum_group(1, far)
     pieces = ((0, near), (1, near), (0, far), (1, far))
@@ -627,13 +653,14 @@
 
     @pl.when(jnp.logical_not(negative))
     def _():
-        up_all.wait_send()
+        for n in range(2):
+            exchanges[n][0].wait_send()
 
     @pl.when(negative)
     def _():
-        down_rest.wait_send()
-        down_first.wait_send()
-        down_last.wait_send()
+        for n in range(2):
+            for copy in exchanges[n][1:]:
+                copy.wait_send()
 
     for copy in started + rs_copies + z_copies + xg_copies:
         copy.wait_send()
@@ -669,11 +696,11 @@
             pltpu.VMEM((tall, SIDE), f32),
             pltpu.VMEM((tall, SIDE), f32),
             pltpu.VMEM((2, HALF, HALF), f32),
-            pltpu.VMEM((2, 8, 16, HALF), f32),
-            pltpu.VMEM((8, 16, HALF), f32),
-            pltpu.VMEM((1, 16, HALF), f32),
-            pltpu.VMEM((8, 16, HALF), f32),
-            pltpu.VMEM((8, 16, HALF), f32),
+            pltpu.VMEM((2, 2, 8, 8, HALF), f32),
+            pltpu.VMEM((2, 8, 8, HALF), f32),
+            pltpu.VMEM((2, 1, 8, HALF), f32),
+            pltpu.VMEM((2, 8, 8, HALF), f32),
+            pltpu.VMEM((2, 8, 8, HALF), f32),
             pltpu.VMEM((LOCAL_TILES, SIDE, SIDE), f32),
             pltpu.VMEM((LOCAL_TILES, 2, 4, WIDTH, SIDE), f32),
             pltpu.VMEM((3, PIECES, WIDTH, SIDE), f32),
@@ -690,10 +717,10 @@
             pltpu.VMEM((LOCAL_PLANES, WIDTH, SIDE), f32),
             dma((LOCAL_PLANES,)),
             dma((7,)),
-            dma((3,)),
-            dma((2,)),
-            dma((31,)),
-            dma((32,)),
+            dma((6,)),
+            dma((4,)),
+            dma((GATHER_SENDS,)),
+            dma((64,)),
             dma((3 * PIECES,)),
             dma((3 * PIECES,)),
             dma((PIECES,)),

time: 64.1 us -> 65.1 us (1.016)
  no operation moved by 1% of the time
where the time goes in v6:
time: 65.1 us; the launch traced here: 64.5 us
  Pallas kernels  62.4 us (96%)
  local copies, waits for them, and re-layouts  2.02 us (3%)
    pallas_call x1, Pallas kernels, on_device(): pl.pallas_call(kernel, name='update', out_shape=jax.ShapeDtypeStruct(volu...  62.4 us
    unnamed x1, local copies, waits for them, and re-layouts  2.02 us

profile of v6, /device:TPU:6, one launch (start us, length us, event | category | flops | bytes accessed | tf_op | source)
XLA Modules:
  0.0 64.5 jit_solution(7321490007373992237)
XLA Ops:
  0.0 62.4 %update.1 = f32[2,8,256,256]{3,2,1,0:T(8,128)S(1)} custom-call(s32[8]{0:T(128)} %phases_hbm.1, s32[64]{0:T(128)} %margins_hbm.1, f32[8,2,8,256]{3,2,1,0:T(8,128)} %transfer_hbm.1, f32[2,8,256,256]{3,2,1,0:T(8,128)} %volume_hbm.1, f32[512,256]{1,0:T(8,128)} %bitcast.2, f32[512,256]{1,0:T(8,128)} %bitcast.3, bf16[8,256,256]{2,1,0:T(8,128)(2,1)} %constant.4.clone.mats_hbm, ...), custom_call_target="tpu_custom_call" | custom-call | tf_op jit(solution)/shard_map/update/pallas_call | solution.py:681
  62.4 2.0 %copy.10 = f32[2,8,256,256]{3,2,1,0:T(8,128)} copy(f32[2,8,256,256]{3,2,1,0:T(8,128)S(1)} %update.1) | data formatting | bytes 8388608

commit v7 on v5

--- a/solution.py
+++ b/solution.py
@@ -16,6 +16,7 @@
 LOCAL_TILES = 2
 LOCAL_PLANES = 8
 PIECES = 4
+EARLY_PLANES = 3
 FLOOR_LEVEL = 0.5
 STEP_GAIN = 2.0
 MESH = pl.DeviceIdType.MESH
@@ -312,7 +313,7 @@
             packed[t, p] = dot3(left(), split(half))
         return carry
 
-    lax.fori_loop(0, LOCAL_PLANES, forward, 0)
+    lax.fori_loop(0, EARLY_PLANES, forward, 0)
 
     @pl.when(jnp.logical_not(negative))
     def _():
@@ -403,6 +404,8 @@
     for dz in z_order:
         pass_on(tile, at(yrow, zlo + dz, core))
     pass_on(tile, sibling)
+
+    lax.fori_loop(EARLY_PLANES, LOCAL_PLANES, forward, 0)
 
     for dz in z_order:
         which = at(yrow, zlo + dz, core)
@@ -611,20 +614,6 @@
 
     lax.fori_loop(0, LOCAL_PLANES, finish_plane, 0)
 
-    def last_strip(p, carry):
-        to_before(p).wait_recv()
-        out[1, p, SIDE - WIDTH :, :] = (1.0 - w_after) * bottom_send[p] + w_after * after_recv[p]
-        return carry
-
-    lax.fori_loop(0, LOCAL_PLANES, last_strip, 0)
-
-    def first_strip(p, carry):
-        to_after(p).wait_recv()
-        out[0, p, :WIDTH, :] = (1.0 - w_before) * before_recv[p] + w_before * top_send[p]
-        return carry
-
-    lax.fori_loop(0, LOCAL_PLANES, first_strip, 0)
-
     @pl.when(jnp.logical_not(negative))
     def _():
         up_all.wait_send()
@@ -637,6 +626,20 @@
 
     for copy in started + rs_copies + z_copies + xg_copies:
         copy.wait_send()
+
+    def last_strip(p, carry):
+        to_before(p).wait_recv()
+        out[1, p, SIDE - WIDTH :, :] = (1.0 - w_after) * bottom_send[p] + w_after * after_recv[p]
+        return carry
+
+    lax.fori_loop(0, LOCAL_PLANES, last_strip, 0)
+
+    def first_strip(p, carry):
+        to_after(p).wait_recv()
+        out[0, p, :WIDTH, :] = (1.0 - w_before) * before_recv[p] + w_before * top_send[p]
+        return carry
+
+    lax.fori_loop(0, LOCAL_PLANES, first_strip, 0)
 
     def drain(p, carry):
         to_before(p).wait_send()

time: 64.1 us -> 63.4 us (0.989)
  Pallas kernels: 62 us -> 61.3 us
    pallas_call x1, Pallas kernels: 62 us -> 61.3 us  [on_device(): pl.pallas_call(kernel, name='update', out_shape=jax.ShapeDtypeStruct(volu...]
where the time goes in v7:
time: 63.4 us; the launch traced here: 63.3 us
  Pallas kernels  61.3 us (97%)
  local copies, waits for them, and re-layouts  2.02 us (3%)
    pallas_call x1, Pallas kernels, on_device(): pl.pallas_call(kernel, name='update', out_shape=jax.ShapeDtypeStruct(volu...  61.3 us
    unnamed x1, local copies, waits for them, and re-layouts  2.02 us

profile of v7, /device:TPU:6, one launch (start us, length us, event | category | flops | bytes accessed | tf_op | source)
XLA Modules:
  0.0 63.3 jit_solution(8584916384779741045)
XLA Ops:
  0.0 61.3 %update.1 = f32[2,8,256,256]{3,2,1,0:T(8,128)S(1)} custom-call(s32[8]{0:T(128)} %phases_hbm.1, s32[64]{0:T(128)} %margins_hbm.1, f32[8,2,8,256]{3,2,1,0:T(8,128)} %transfer_hbm.1, f32[2,8,256,256]{3,2,1,0:T(8,128)} %volume_hbm.1, f32[512,256]{1,0:T(8,128)} %bitcast.2, f32[512,256]{1,0:T(8,128)} %bitcast.3, bf16[8,256,256]{2,1,0:T(8,128)(2,1)} %constant.4.clone.mats_hbm, ...), custom_call_target="tpu_custom_call" | custom-call | tf_op jit(solution)/shard_map/update/pallas_call | solution.py:657
  61.3 2.0 %copy.10 = f32[2,8,256,256]{3,2,1,0:T(8,128)} copy(f32[2,8,256,256]{3,2,1,0:T(8,128)S(1)} %update.1) | data formatting | bytes 8388608

commit v8 on v7

--- a/solution.py
+++ b/solution.py
@@ -399,10 +399,10 @@
     below = at(yrow + 3, zlo, core)
     sibling = at(yrow, zlo, 1 - core)
     z_order = (1, 3, 2)
+    for dz in z_order:
+        pass_on(tile, at(yrow, zlo + dz, core))
     pass_on(tile, above)
     pass_on(tile, below)
-    for dz in z_order:
-        pass_on(tile, at(yrow, zlo + dz, core))
     pass_on(tile, sibling)
 
     lax.fori_loop(EARLY_PLANES, LOCAL_PLANES, forward, 0)

time: 63.4 us -> 63.4 us (level)
  no operation moved by 1% of the time
where the time goes in v8:
time: 63.4 us; the launch traced here: 63.3 us
  Pallas kernels  61.3 us (97%)
  local copies, waits for them, and re-layouts  2.02 us (3%)
    pallas_call x1, Pallas kernels, on_device(): pl.pallas_call(kernel, name='update', out_shape=jax.ShapeDtypeStruct(volu...  61.3 us
    unnamed x1, local copies, waits for them, and re-layouts  2.02 us

profile of v8, /device:TPU:6, one launch (start us, length us, event | category | flops | bytes accessed | tf_op | source)
XLA Modules:
  0.0 63.3 jit_solution(11817192609719239205)
XLA Ops:
  0.0 61.3 %update.1 = f32[2,8,256,256]{3,2,1,0:T(8,128)S(1)} custom-call(s32[8]{0:T(128)} %phases_hbm.1, s32[64]{0:T(128)} %margins_hbm.1, f32[8,2,8,256]{3,2,1,0:T(8,128)} %transfer_hbm.1, f32[2,8,256,256]{3,2,1,0:T(8,128)} %volume_hbm.1, f32[512,256]{1,0:T(8,128)} %bitcast.2, f32[512,256]{1,0:T(8,128)} %bitcast.3, bf16[8,256,256]{2,1,0:T(8,128)(2,1)} %constant.4.clone.mats_hbm, ...), custom_call_target="tpu_custom_call" | custom-call | tf_op jit(solution)/shard_map/update/pallas_call | solution.py:657
  61.3 2.0 %copy.10 = f32[2,8,256,256]{3,2,1,0:T(8,128)} copy(f32[2,8,256,256]{3,2,1,0:T(8,128)S(1)} %update.1) | data formatting | bytes 8388608
